TPU v7x, 128 devices: a whole 4x4x4 slice. The times are simulated.
128 devices in a mesh: rep: 1, r: 4 (over x), s: 32 (over y, z, core).
Axes of the slice: x: 4, y: 4, z: 4, core: 2. Of those that a mesh axis runs over, the one named last changes fastest.
Arguments:
- x: bfloat16 [128, 2048, 1024], P(('rep', 'r', 's'))
- dy: bfloat16 [128, 2048, 1024], P(('rep', 'r', 's'))
- w_gate: bfloat16 [2, 1024, 3328], P(None, 's')
- w_up: bfloat16 [2, 1024, 3328], P(None, 's')
- w_down: bfloat16 [2, 3328, 1024], P(None, 's')
- m_w_gate: float32 [2, 1024, 3328], P(None, 's')
- m_w_up: float32 [2, 1024, 3328], P(None, 's')
- m_w_down: float32 [2, 3328, 1024], P(None, 's')
- v_w_gate: float32 [2, 1024, 3328], P(None, 's')
- v_w_up: float32 [2, 1024, 3328], P(None, 's')
- v_w_down: float32 [2, 3328, 1024], P(None, 's')
Outputs:
- output 1: bfloat16 [2, 1024, 3328], P('rep', 's')
- output 2: bfloat16 [2, 1024, 3328], P('rep', 's')
- output 3: bfloat16 [2, 3328, 1024], P('rep', 's')
- output 4: float32 [2, 1024, 3328], P('rep', 's')
- output 5: float32 [2, 1024, 3328], P('rep', 's')
- output 6: float32 [2, 3328, 1024], P('rep', 's')
- output 7: float32 [2, 1024, 3328], P('rep', 's')
- output 8: float32 [2, 1024, 3328], P('rep', 's')
- output 9: float32 [2, 3328, 1024], P('rep', 's')
All inputs are finite; a program needn't handle non-finite values.
Results may differ from a plain program's by a relative error of at most 0.022.
Values are sent between devices in bfloat16 or wider.
A program may use at most 1.5 GiB of HBM per device.

v0:
```python
import jax
import jax.numpy as jnp
from jax import lax
from jax.sharding import PartitionSpec as P

NAMES = ("w_gate", "w_up", "w_down")


def matmul(a, w):
    return jnp.dot(a, w, preferred_element_type=jnp.float32).astype(jnp.bfloat16)


def normed(h):
    wide = h.astype(jnp.float32)
    scale = lax.rsqrt(jnp.mean(wide**2, -1, keepdims=True) + 1e-6)
    return (wide * scale).astype(jnp.bfloat16)


def layer(h, w):
    a = normed(h)
    gate = jnp.dot(a, w["w_gate"], preferred_element_type=jnp.float32)
    up = jnp.dot(a, w["w_up"], preferred_element_type=jnp.float32)
    return h + matmul((jax.nn.silu(gate) * up).astype(jnp.bfloat16), w["w_down"])


def adamw(w, m, v, g):
    m = 0.9 * m + 0.1 * g
    v = 0.95 * v + 0.05 * g * g
    step = m * lax.rsqrt(v + 1e-8) + 0.1 * w
    return (w - 0.02 * step).astype(jnp.bfloat16), m, v


def solution(mesh):
    def fetched(weights, number):
        return {name: lax.all_gather(w[number], "s", axis=0, tiled=True) for name, w in zip(NAMES, weights, strict=True)}

    def summed(term):
        return lax.psum(lax.psum_scatter(term, "s", scatter_dimension=0, tiled=True), "r")

    def step(x, dy, *arrays):
        weights, m, v = (arrays[i : i + 3] for i in (0, 3, 6))
        layers = weights[0].shape[0]
        h, kept = x[0], []
        for number in range(layers):
            kept.append(h)
            h = layer(h, fetched(weights, number))
        by_h, mine = dy[0], [None] * layers
        for number in reversed(range(layers)):
            _, back = jax.vjp(lambda w, h: layer(h, w), fetched(weights, number), kept[number])
            by_w, by_h = back(by_h)
            mine[number] = [summed(by_w[name]) for name in NAMES]
        gradients = [jnp.stack([mine[number][i] for number in range(layers)]).astype(jnp.float32) for i in range(3)]
        new = [adamw(w.astype(jnp.float32), m, v, g) for w, m, v, g in zip(weights, m, v, gradients, strict=True)]
        return tuple(one[which] for which in range(3) for one in new)

    states, cut = P(("rep", "r", "s"), None, None), P(None, "s", None)
    return jax.shard_map(
        step,
        mesh=mesh,
        in_specs=(states, states) + (cut,) * 9,
        out_specs=(P("rep", "s", None),) * 9,
        check_vma=False,
    )
```

profile of v0, /device:TPU:0, one launch (start us, length us, event | category | flops | bytes accessed | tf_op | source)
XLA Modules:
  0.0 1033.3 jit_solution(1566847433298776208)
XLA Ops:
  7.2 0.0 all-gather.13.cloned.1.call-start
  7.2 1.8 fusion.88
  9.0 0.0 all-gather.13.cloned.1.call-update
  9.1 0.0 all-gather.15.cloned.1.call-start
  9.1 1.8 fusion.87
  10.9 0.0 all-gather.15.cloned.1.call-update
  11.0 0.0 all-gather.17.cloned.1.call-start
  11.0 1.8 fusion.86
  12.8 0.0 all-gather.17.cloned.1.call-update
  12.8 0.0 all-gather.23.cloned.1.call-start
  12.9 0.5 all-gather.23.cloned.1.call-update
  13.4 0.0 all-gather.21.cloned.1.call-start
  13.5 0.5 all-gather.21.cloned.1.call-update
  14.0 0.0 all-gather.19.cloned.1.call-start
  14.1 0.5 all-gather.19.cloned.1.call-update
  14.6 0.0 reduce-scatter.15.cloned.1.call-start
  14.6 6.5 copy.20
  21.2 3.1 fusion.15
  24.3 6.6 copy.21
  30.8 32.5 %all-gather.13.cloned.1.call-done = bf16[1,1024,3328]{2,1,0:T(8,128)(2,1)} async-done(((bf16[1,32,3328]{2,1,0:T(8,128)(2,1)}), bf16[1,1024,3328]{2,1,0:T(8,128)(2,1)}) %all-gather.13.cloned.1.call-update) | async-done | bytes 6815760 | tf_op jit(solution)/shard_map/all_gather | solution.py:35
  63.3 23.2 %fusion.41 = f32[2048,3328]{1,0:T(8,128)} fusion(bf16[1,1024,3328]{2,1,0:T(8,128)(2,1)} %all-gather.13.cloned.1.call-done, bf16[1,2048,1024]{1,2,0:T(8,128)(2,1)} %copy.20, f32[2048]{0:T(1024)S(1)} %add_rsqrt_fusion), kind=kOutput, calls=%fused_computation.59 | convolution fusion | flops 13964935168 | bytes 38281216 | tf_op jit(solution)/shard_map/dot_general | solution.py:21
  86.5 28.3 %all-gather.15.cloned.1.call-done = bf16[1,1024,3328]{2,1,0:T(8,128)(2,1)} async-done(((bf16[1,32,3328]{2,1,0:T(8,128)(2,1)}), bf16[1,1024,3328]{2,1,0:T(8,128)(2,1)}) %all-gather.15.cloned.1.call-update) | async-done | bytes 6815760 | tf_op jit(solution)/shard_map/all_gather | solution.py:35
  114.8 32.1 %multiply_convert_fusion.1 = (bf16[2048,3328]{1,0:T(8,128)(2,1)}, f32[2048,3328]{1,0:T(8,128)}) fusion(f32[2048,3328]{1,0:T(8,128)} %fusion.41, bf16[1,1024,3328]{2,1,0:T(8,128)(2,1)} %all-gather.15.cloned.1.call-done, bf16[1,2048,1024]{1,2,0:T(8,128)(2,1)} %copy.20, f32[2048]{0:T(1024)S(1)} %add_rsqrt_fusion), kind=kOutput, calls=%fused_computation.17 | convolution fusion | flops 14005829632 | bytes 79175680 | tf_op jit(solution)/shard_map/dot_general | solution.py:22
  147.0 19.4 %all-gather.17.cloned.1.call-done = bf16[1,3328,1024]{2,1,0:T(8,128)(2,1)} async-done(((bf16[1,104,1024]{2,1,0:T(8,128)(2,1)}), bf16[1,3328,1024]{2,1,0:T(8,128)(2,1)}) %all-gather.17.cloned.1.call-update) | async-done | bytes 6815760 | tf_op jit(solution)/shard_map/all_gather | solution.py:35
  166.3 22.1 %fusion.19 = (f32[2048]{0:T(1024)S(1)}, bf16[2048,1024]{0,1:T(8,128)(2,1)}) fusion(bf16[2048,3328]{1,0:T(8,128)(2,1)} %get-tuple-element.30, bf16[1,3328,1024]{2,1,0:T(8,128)(2,1)} %all-gather.17.cloned.1.call-done, bf16[1,2048,1024]{1,2,0:T(8,128)(2,1)} %copy.20), kind=kOutput, calls=%fused_computation.37 | convolution fusion | flops 13969127424 | bytes 28844032 | tf_op jit(solution)/shard_map/dot_general | solution.py:10
  188.5 29.2 %all-gather.23.cloned.1.call-done = bf16[1,1024,3328]{2,1,0:T(8,128)(2,1)} async-done(((bf16[1,32,3328]{2,1,0:T(8,128)(2,1)}), bf16[1,1024,3328]{2,1,0:T(8,128)(2,1)}) %all-gather.23.cloned.1.call-update) | async-done | bytes 6815760 | tf_op jit(solution)/shard_map/all_gather | solution.py:35
  217.7 23.5 %fusion.28 = f32[2048,3328]{1,0:T(8,128)} fusion(bf16[1,1024,3328]{2,1,0:T(8,128)(2,1)} %all-gather.23.cloned.1.call-done, bf16[2048,1024]{0,1:T(8,128)(2,1)} %get-tuple-element.33, f32[2048]{0:T(1024)S(1)} %fusion.74), kind=kOutput, calls=%fused_computation.46 | convolution fusion | flops 13964935168 | bytes 38281216 | tf_op jit(solution)/shard_map/jvp()/dot_general | solution.py:22
  241.2 27.8 %all-gather.21.cloned.1.call-done = bf16[1,3328,1024]{2,1,0:T(8,128)(2,1)} async-done(((bf16[1,104,1024]{2,1,0:T(8,128)(2,1)}), bf16[1,3328,1024]{2,1,0:T(8,128)(2,1)}) %all-gather.21.cloned.1.call-update) | async-done | bytes 6815760 | tf_op jit(solution)/shard_map/all_gather | solution.py:35
  269.0 21.0 %convolution_convert_fusion.1 = bf16[2048,3328]{1,0:T(8,128)(2,1)} fusion(bf16[1,3328,1024]{2,1,0:T(8,128)(2,1)} %all-gather.21.cloned.1.call-done, bf16[1,2048,1024]{2,1,0:T(8,128)(2,1)} %param.12), kind=kOutput, calls=%fused_computation.23 | convolution fusion | flops 13965459456 | bytes 24641536 | tf_op jit(solution)/shard_map/transpose(jvp())/dot_general | solution.py:10
  290.0 30.4 %all-gather.19.cloned.1.call-done = bf16[1,1024,3328]{2,1,0:T(8,128)(2,1)} async-done(((bf16[1,32,3328]{2,1,0:T(8,128)(2,1)}), bf16[1,1024,3328]{2,1,0:T(8,128)(2,1)}) %all-gather.19.cloned.1.call-update) | async-done | bytes 6815760 | tf_op jit(solution)/shard_map/all_gather | solution.py:35
  320.3 39.6 %fusion.2 = (bf16[2048,3328]{1,0:T(8,128)(2,1)}, f32[2048,3328]{1,0:T(8,128)}) fusion(f32[2048,3328]{1,0:T(8,128)} %fusion.28, bf16[2048,3328]{1,0:T(8,128)(2,1)} %convolution_convert_fusion.1, bf16[1,1024,3328]{2,1,0:T(8,128)(2,1)} %all-gather.19.cloned.1.call-done, bf16[2048,1024]{0,1:T(8,128)(2,1)} %get-tuple-element.33, f32[2048]{0:T(1024)S(1)} %fusion.74), kind=kOutput, calls=%fused_computation.8 | convolution fusion | flops 14046724096 | bytes 92807168 | tf_op jit(solution)/shard_map/jvp()/dot_general | solution.py:21
  360.0 23.1 %fusion.12 = bf16[2048,1024]{0,1:T(8,128)(2,1)} fusion(bf16[2048,3328]{1,0:T(8,128)(2,1)} %convolution_convert_fusion.1, bf16[1,1024,3328]{2,1,0:T(8,128)(2,1)} %all-gather.23.cloned.1.call-done, f32[2048,3328]{1,0:T(8,128)} %get-tuple-element.35), kind=kOutput, calls=%fused_computation.21 | convolution fusion | flops 13999538176 | bytes 51904512 | tf_op jit(solution)/shard_map/transpose(jvp())/dot_general | solution.py:22
  383.1 21.7 %fusion.21 = (f32[2048]{0:T(1024)S(1)}, bf16[2048,1024]{0,1:T(8,128)(2,1)}) fusion(bf16[2048,1024]{0,1:T(8,128)(2,1)S(1)} %copy-done.1, bf16[2048,1024]{0,1:T(8,128)(2,1)} %fusion.12, bf16[2048,3328]{1,0:T(8,128)(2,1)} %get-tuple-element.34, bf16[1,1024,3328]{2,1,0:T(8,128)(2,1)} %all-gather.19.cloned.1.call-done), kind=kOutput, calls=%fused_computation.39 | convolution fusion | flops 13969127424 | bytes 33038336 | tf_op jit(solution)/shard_map/transpose(jvp())/dot_general | solution.py:21
  404.9 4.9 fusion.44
  409.8 2.0 copy-done.2
  411.7 19.6 %convolution_convert_fusion.2 = bf16[3328,1024]{1,0:T(8,128)(2,1)} fusion(bf16[2048,3328]{1,0:T(8,128)(2,1)} %get-tuple-element.30, bf16[2048,1024]{0,1:T(8,128)(2,1)S(1)} %fusion.44), kind=kOutput, calls=%fused_computation.44 | convolution fusion | flops 13962051584 | bytes 24641536 | tf_op jit(solution)/shard_map/transpose(jvp())/dot_general | solution.py:10
  431.3 0.0 reduce-scatter.15.cloned.1.call-update
  431.4 0.0 reduce-scatter.17.cloned.1.call-start
  431.4 27.4 %fusion.25 = bf16[3328,1024]{1,0:T(8,128)(2,1)} fusion(f32[2048,3328]{1,0:T(8,128)} %fusion.28, bf16[1,2048,1024]{2,1,0:T(8,128)(2,1)} %param.12, f32[2048,3328]{1,0:T(8,128)} %get-tuple-element.35), kind=kOutput, calls=%fused_computation.41 | convolution fusion | flops 14002946048 | bytes 65536000 | tf_op jit(solution)/shard_map/transpose(jvp())/dot_general | solution.py:10
  458.8 0.0 reduce-scatter.17.cloned.1.call-update
  458.9 0.0 reduce-scatter.11.cloned.1.call-start
  458.9 21.1 %convolution_convert_fusion = bf16[2048,3328]{1,0:T(8,128)(2,1)} fusion(bf16[2048,1024]{0,1:T(8,128)(2,1)} %copy-done.2, bf16[1,3328,1024]{2,1,0:T(8,128)(2,1)} %all-gather.17.cloned.1.call-done), kind=kOutput, calls=%fused_computation.22 | convolution fusion | flops 13965459456 | bytes 24641536 | tf_op jit(solution)/shard_map/transpose(jvp())/dot_general | solution.py:10
  480.0 25.6 %fusion.27 = bf16[1024,3328]{1,0:T(8,128)(2,1)} fusion(bf16[2048,3328]{1,0:T(8,128)(2,1)} %convolution_convert_fusion, f32[2048,3328]{1,0:T(8,128)} %fusion.41, bf16[1,2048,1024]{1,2,0:T(8,128)(2,1)} %copy.20, f32[2048]{0:T(1024)S(1)} %copy-done.13), kind=kOutput, calls=%fused_computation.43 | convolution fusion | flops 14009237504 | bytes 51912704 | tf_op jit(solution)/shard_map/transpose(jvp())/dot_general | solution.py:22
  505.6 0.0 reduce-scatter.11.cloned.1.call-update
  505.6 0.0 reduce-scatter.13.cloned.1.call-start
  505.7 25.3 %fusion.26 = bf16[1024,3328]{1,0:T(8,128)(2,1)} fusion(bf16[2048,3328]{1,0:T(8,128)(2,1)} %convolution_convert_fusion.1, bf16[2048,1024]{0,1:T(8,128)(2,1)} %get-tuple-element.33, f32[2048]{0:T(1024)S(1)} %copy-done.9, f32[2048,3328]{1,0:T(8,128)} %get-tuple-element.35), kind=kOutput, calls=%fused_computation.42 | convolution fusion | flops 14009237504 | bytes 51912704 | tf_op jit(solution)/shard_map/transpose(jvp())/dot_general | solution.py:22
  531.0 0.0 reduce-scatter.13.cloned.1.call-update
  531.0 0.0 reduce-scatter.7.cloned.1.call-start
  531.0 31.3 %fusion.22 = bf16[1024,3328]{1,0:T(8,128)(2,1)} fusion(f32[2048,3328]{1,0:T(8,128)} %fusion.41, f32[2048,3328]{1,0:T(8,128)} %get-tuple-element.31, bf16[2048,3328]{1,0:T(8,128)(2,1)} %convolution_convert_fusion, bf16[1,2048,1024]{1,2,0:T(8,128)(2,1)} %copy.20, f32[2048]{0:T(1024)S(1)} %copy-done.13), kind=kOutput, calls=%fused_computation.40 | convolution fusion | flops 14043316224 | bytes 79175680 | tf_op jit(solution)/shard_map/transpose(jvp())/dot_general | solution.py:21
  562.3 0.0 reduce-scatter.7.cloned.1.call-update
  562.3 0.0 reduce-scatter.9.cloned.1.call-start
  562.4 21.3 %convolution_convert_fusion.3 = bf16[1024,3328]{1,0:T(8,128)(2,1)} fusion(bf16[2048,3328]{1,0:T(8,128)(2,1)} %get-tuple-element.34, bf16[2048,1024]{0,1:T(8,128)(2,1)} %get-tuple-element.33, f32[2048]{0:T(1024)S(1)} %copy-done.9), kind=kOutput, calls=%fused_computation.45 | convolution fusion | flops 13964935168 | bytes 24649728 | tf_op jit(solution)/shard_map/transpose(jvp())/dot_general | solution.py:21
  583.7 0.0 reduce-scatter.9.cloned.1.call-update
  583.7 0.0 all-reduce.3.cloned.1.call-start
  583.7 0.0 reduce-scatter.15.cloned.1.call-done
  583.8 24.2 %reduce-scatter.17.cloned.1.call-done = bf16[104,1024]{1,0:T(8,128)(2,1)} async-done(((bf16[3328,1024]{1,0:T(8,128)(2,1)}), bf16[104,1024]{1,0:T(8,128)(2,1)}) %reduce-scatter.17.cloned.1.call-update) | async-done | bytes 213008 | tf_op jit(solution)/shard_map/reduce_scatter | solution.py:38
  607.9 90.4 %reduce-scatter.11.cloned.1.call-done = bf16[32,3328]{1,0:T(8,128)(2,1)} async-done(((bf16[1024,3328]{1,0:T(8,128)(2,1)}), bf16[32,3328]{1,0:T(8,128)(2,1)}) %reduce-scatter.11.cloned.1.call-update) | async-done | bytes 213008 | tf_op jit(solution)/shard_map/reduce_scatter | solution.py:38
  698.3 90.3 %reduce-scatter.13.cloned.1.call-done = bf16[32,3328]{1,0:T(8,128)(2,1)} async-done(((bf16[1024,3328]{1,0:T(8,128)(2,1)}), bf16[32,3328]{1,0:T(8,128)(2,1)}) %reduce-scatter.13.cloned.1.call-update) | async-done | bytes 213008 | tf_op jit(solution)/shard_map/reduce_scatter | solution.py:38
  788.6 90.4 %reduce-scatter.7.cloned.1.call-done = bf16[32,3328]{1,0:T(8,128)(2,1)} async-done(((bf16[1024,3328]{1,0:T(8,128)(2,1)}), bf16[32,3328]{1,0:T(8,128)(2,1)}) %reduce-scatter.7.cloned.1.call-update) | async-done | bytes 213008 | tf_op jit(solution)/shard_map/reduce_scatter | solution.py:38
  879.1 90.3 %reduce-scatter.9.cloned.1.call-done = bf16[32,3328]{1,0:T(8,128)(2,1)} async-done(((bf16[1024,3328]{1,0:T(8,128)(2,1)}), bf16[32,3328]{1,0:T(8,128)(2,1)}) %reduce-scatter.9.cloned.1.call-update) | async-done | bytes 213008 | tf_op jit(solution)/shard_map/reduce_scatter | solution.py:38
  969.4 0.0 all-reduce.3.cloned.1.call-update
  969.4 49.6 %all-reduce.3.cloned.1.call-done = (bf16[1,32,3328]{2,1,0:T(8,128)(2,1)}, bf16[1,32,3328]{2,1,0:T(8,128)(2,1)}, bf16[1,32,3328]{2,1,0:T(8,128)(2,1)}, bf16[1,32,...) async-done(((bf16[1,32,3328]{2,1,0:T(8,128)(2,1)}, bf16[1,32,3328]{2,1,0:T(8,128)(2,1)}, bf16[1,32,3328]{2,1,0:T(8,128)(2,1)}, ...) | async-done | bytes 1277968 | tf_op jit(solution)/shard_map/psum | solution.py:38
  1019.0 2.6 fusion.69
  1021.6 4.7 fusion.61
  (30 shorter events, 0.1 us)
Async XLA Ops:
  7.2 56.2 %all-gather.13.cloned.1.call-start = ((), (), s32[]{:S(2)}) async-start(), calls=%async_computation.12 | async-start | bytes 7028736 | tf_op jit(solution)/shard_map/all_gather | solution.py:35
  9.1 105.8 %all-gather.15.cloned.1.call-start = ((), (), s32[]{:S(2)}) async-start(), calls=%async_computation.13 | async-start | bytes 7028736 | tf_op jit(solution)/shard_map/all_gather | solution.py:35
  11.0 155.4 %all-gather.17.cloned.1.call-start = ((), (), s32[]{:S(2)}) async-start(), calls=%async_computation.14 | async-start | bytes 7028736 | tf_op jit(solution)/shard_map/all_gather | solution.py:35
  12.8 204.8 %all-gather.23.cloned.1.call-start = ((), (), s32[]{:S(2)}) async-start(), calls=%async_computation.17 | async-start | bytes 7028736 | tf_op jit(solution)/shard_map/all_gather | solution.py:35
  13.4 255.6 %all-gather.21.cloned.1.call-start = ((), (), s32[]{:S(2)}) async-start(), calls=%async_computation.16 | async-start | bytes 7028736 | tf_op jit(solution)/shard_map/all_gather | solution.py:35
  14.0 306.3 %all-gather.19.cloned.1.call-start = ((), (), s32[]{:S(2)}) async-start(), calls=%async_computation.15 | async-start | bytes 7028736 | tf_op jit(solution)/shard_map/all_gather | solution.py:35
  14.6 569.2 %reduce-scatter.15.cloned.1.call-start = ((), (), s32[]{:S(2)}) async-start(), calls=%async_computation.10 | async-start | bytes 7028736 | tf_op jit(solution)/shard_map/reduce_scatter | solution.py:38
  24.2 90.6 %copy-start.12 = (f32[2048]{0:T(1024)}, f32[2048]{0:T(1024)S(1)}, u32[]{:S(2)}) copy-start(f32[2048]{0:T(1024)S(1)} %add_rsqrt_fusion) | copy-start | bytes 24580
  188.5 52.7 %copy-start.10 = (f32[2048]{0:T(1024)}, f32[2048]{0:T(1024)S(1)}, u32[]{:S(2)}) copy-start(f32[2048]{0:T(1024)S(1)} %get-tuple-element.32) | copy-start | bytes 24580
  188.5 216.4 %copy-start.8 = (f32[2048]{0:T(1024)}, f32[2048]{0:T(1024)S(1)}, u32[]{:S(2)}) copy-start(f32[2048]{0:T(1024)S(1)} %fusion.74) | copy-start | bytes 24580
  360.0 23.1 %copy-start.1 = (bf16[2048,1024]{0,1:T(8,128)(2,1)S(1)}, bf16[2048,1024]{0,1:T(8,128)(2,1)}, u32[]{:S(2)}) copy-start(bf16[2048,1024]{0,1:T(8,128)(2,1)} %get-tuple-element.33) | copy-start | bytes 12582916
  383.1 21.7 %copy-start.11 = (f32[2048]{0:T(1024)S(1)}, f32[2048]{0:T(1024)}, u32[]{:S(2)}) copy-start(f32[2048]{0:T(1024)} %copy-done.10) | copy-start | bytes 24580
  383.1 21.8 %copy-start = (bf16[1,2048,1024]{1,2,0:T(8,128)(2,1)S(1)}, bf16[1,2048,1024]{1,2,0:T(8,128)(2,1)}, u32[]{:S(2)}) copy-start(bf16[1,2048,1024]{1,2,0:T(8,128)(2,1)} %copy.21) | copy-start | bytes 12582916
  409.8 2.0 copy-start.2
  431.4 176.6 %reduce-scatter.17.cloned.1.call-start = ((), (), s32[]{:S(2)}) async-start(), calls=%async_computation.11 | async-start | bytes 7028736 | tf_op jit(solution)/shard_map/reduce_scatter | solution.py:38
  458.9 21.1 %copy-start.13 = (f32[2048]{0:T(1024)S(1)}, f32[2048]{0:T(1024)}, u32[]{:S(2)}) copy-start(f32[2048]{0:T(1024)} %copy-done.12) | copy-start | bytes 24580
  458.9 239.5 %reduce-scatter.11.cloned.1.call-start = ((), (), s32[]{:S(2)}) async-start(), calls=%async_computation.8 | async-start | bytes 7028736 | tf_op jit(solution)/shard_map/reduce_scatter | solution.py:38
  480.0 25.7 %copy-start.9 = (f32[2048]{0:T(1024)S(1)}, f32[2048]{0:T(1024)}, u32[]{:S(2)}) copy-start(f32[2048]{0:T(1024)} %copy-done.8) | copy-start | bytes 24580
  505.6 283.0 %reduce-scatter.13.cloned.1.call-start = ((), (), s32[]{:S(2)}) async-start(), calls=%async_computation.9 | async-start | bytes 7028736 | tf_op jit(solution)/shard_map/reduce_scatter | solution.py:38
  531.0 348.1 %reduce-scatter.7.cloned.1.call-start = ((), (), s32[]{:S(2)}) async-start(), calls=%async_computation.6 | async-start | bytes 7028736 | tf_op jit(solution)/shard_map/reduce_scatter | solution.py:38
  562.3 407.1 %reduce-scatter.9.cloned.1.call-start = ((), (), s32[]{:S(2)}) async-start(), calls=%async_computation.7 | async-start | bytes 7028736 | tf_op jit(solution)/shard_map/reduce_scatter | solution.py:38
  583.6 435.4 %copy-start.3 = (bf16[2,104,1024]{2,1,0:T(8,128)(2,1)S(1)}, bf16[2,104,1024]{2,1,0:T(8,128)(2,1)}, u32[]{:S(2)}) copy-start(bf16[2,104,1024]{2,1,0:T(8,128)(2,1)} %param.15) | copy-start | bytes 1277956
  583.6 435.4 %copy-start.6 = (f32[2,104,1024]{2,1,0:T(8,128)S(1)}, f32[2,104,1024]{2,1,0:T(8,128)}, u32[]{:S(2)}) copy-start(f32[2,104,1024]{2,1,0:T(8,128)} %param.21) | copy-start | bytes 2555908
  583.6 435.4 %copy-start.7 = (f32[2,104,1024]{2,1,0:T(8,128)S(1)}, f32[2,104,1024]{2,1,0:T(8,128)}, u32[]{:S(2)}) copy-start(f32[2,104,1024]{2,1,0:T(8,128)} %param.18) | copy-start | bytes 2555908
  583.6 438.0 %copy-start.4 = (bf16[2,32,3328]{2,1,0:T(8,128)(2,1)S(1)}, bf16[2,32,3328]{2,1,0:T(8,128)(2,1)}, u32[]{:S(2)}) copy-start(bf16[2,32,3328]{2,1,0:T(8,128)(2,1)} %param.13) | copy-start | bytes 1277956
  583.7 438.0 %copy-start.5 = (bf16[2,32,3328]{2,1,0:T(8,128)(2,1)S(1)}, bf16[2,32,3328]{2,1,0:T(8,128)(2,1)}, u32[]{:S(2)}) copy-start(bf16[2,32,3328]{2,1,0:T(8,128)(2,1)} %param.14) | copy-start | bytes 1277956
  583.7 435.3 %all-reduce.3.cloned.1.call-start = ((), (), s32[]{:S(2)}) async-start(), calls=%async_computation.18 | async-start | bytes 2555904 | tf_op jit(solution)/shard_map/psum | solution.py:38
Sparse Core Ops, SparseCore 0:
  10.8 52.4 all-gather.12
  66.2 48.6 all-gather.14
  117.7 48.6 all-gather.16
  169.0 48.6 all-gather.22
  220.3 48.6 all-gather.20
  271.7 48.6 all-gather.18
  431.5 85.9 reduce-scatter.14
  521.3 86.5 reduce-scatter.16
  611.7 86.5 reduce-scatter.10
  702.0 86.6 reduce-scatter.12
  792.4 86.6 reduce-scatter.6
  882.7 86.6 reduce-scatter.8
  972.2 46.8 all-reduce.2
where the time goes:
time: 1040 us; the launch traced here: 1030 us
  waiting for transfers between devices  605 us (58%)
  matrix products  378 us (36%)
  local copies, waits for them, and re-layouts  20.6 us (2%)
  other arithmetic  15.2 us (1%)
  between operations  14.5 us (1%)
    reduce_scatter x6, waiting for transfers between devices, summed(): lax.psum_scatter(term, 's', scatter_dimension=0, tiled=True)  386 us
    all_gather x6, waiting for transfers between devices, fetched(): lax.all_gather(w[number], 's', axis=0, tiled=True)  168 us
    dot_general x5, matrix products, layer(): gate = jnp.dot(a, w['w_gate'], preferred_element_type=jnp.float32)  137 us
    dot_general x5, matrix products, layer(): up = jnp.dot(a, w['w_up'], preferred_element_type=jnp.float32)  130 us
    dot_general x5, matrix products, matmul(): jnp.dot(a, w, preferred_element_type=jnp.float32).astype(jnp.bfloat16)  111 us
    psum x1, waiting for transfers between devices, summed(): lax.psum(lax.psum_scatter(term, 's', scatter_dimension=0, tiled=True), 'r')  49.6 us
  transfers between devices with their start and end apart: 13, of which 12 were waited for; matrix products, arithmetic and copies ran while one was open for 28% of the time, Pallas kernels for 0%

commit v1 on v0

v1 whole, which is shorter than its diff:
```python
import functools

import jax
import jax.numpy as jnp
from jax import lax
from jax.experimental import pallas as pl
from jax.experimental.pallas import tpu as pltpu
from jax.sharding import PartitionSpec as P

NAMES = ("w_gate", "w_up", "w_down")
MESH = pl.DeviceIdType.MESH
F32, BF16 = jnp.float32, jnp.bfloat16
HOPS = 6


def matmul(a, w):
    return jnp.dot(a, w, preferred_element_type=jnp.float32).astype(jnp.bfloat16)


def normed(h):
    wide = h.astype(jnp.float32)
    scale = lax.rsqrt(jnp.mean(wide**2, -1, keepdims=True) + 1e-6)
    return (wide * scale).astype(jnp.bfloat16)


def layer(h, w):
    a = normed(h)
    gate = jnp.dot(a, w["w_gate"], preferred_element_type=jnp.float32)
    up = jnp.dot(a, w["w_up"], preferred_element_type=jnp.float32)
    return h + matmul((jax.nn.silu(gate) * up).astype(jnp.bfloat16), w["w_down"])


def adamw(w, m, v, g):
    m = 0.9 * m + 0.1 * g
    v = 0.95 * v + 0.05 * g * g
    step = m * lax.rsqrt(v + 1e-8) + 0.1 * w
    return (w - 0.02 * step).astype(jnp.bfloat16), m, v


class Place:
    def __init__(self):
        self.s, self.x = lax.axis_index("s"), lax.axis_index("r")
        self.core = self.s % 2
        y, z = self.s // 8, (self.s // 2) % 4
        self.a = y * (1 - self.core) + z * self.core
        self.b = z * (1 - self.core) + y * self.core
        self.step_a, self.step_b = 8 - 6 * self.core, 2 + 6 * self.core

    def chip(self, a, b):
        return (a % 4) * (self.step_a // 2) + (b % 4) * (self.step_b // 2)

    def at(self, a, b):
        return {"s": 2 * self.chip(a, b) + self.core}

    def partner(self):
        return {"s": self.s + 1 - 2 * self.core}

    def along_x(self, d):
        return {"r": (self.x + d) % 4}

    def neighbours(self):
        a, b = self.a, self.b
        plane = [self.partner()] + [self.at(a + d, b) for d in (1, 3)] + [self.at(a, b + d) for d in (1, 3)]
        return plane + [self.along_x(d) for d in (1, 2, 3)]


def meet(places):
    barrier = pltpu.get_barrier_semaphore()
    for place in places:
        pl.semaphore_signal(barrier, inc=1, device_id=place, device_id_type=MESH)
    pl.semaphore_wait(barrier, len(places))


def send(src, dst, send_sem, recv_sem, place):
    return pltpu.make_async_remote_copy(src_ref=src, dst_ref=dst, send_sem=send_sem, recv_sem=recv_sem, device_id=place, device_id_type=MESH)


def gather_kernel(layers, *refs):
    n = 3 * layers
    shards, full = refs[:3], refs[3 : 3 + n]
    here = refs[3 + n : 6 + n]
    sems_out, sems_in, sems_here = refs[6 + n :]
    p = Place()
    meet(p.neighbours()[:5])
    loads = [pltpu.make_async_copy(shards[i], here[i], sems_here.at[i]) for i in range(3)]
    for load in loads:
        load.start()
    for load in loads:
        load.wait()

    def run(core):
        def group(m, b, columns=None):
            whole = full[m].at[:, b % 4, core] if core == 0 else full[m].at[b % 4, :, core]
            return whole if columns is None else whole.at[:, :, pl.ds(*columns)]

        def piece(m, a, b, columns=None):
            whole = full[m].at[a % 4, b % 4, core] if core == 0 else full[m].at[b % 4, a % 4, core]
            return whole if columns is None else whole.at[:, pl.ds(*columns)]

        a, b = p.a, p.b
        started = []

        def go(m, i, src, dst, place):
            copy = send(src, dst, sems_out.at[m, i], sems_in.at[m, i], place)
            copy.start()
            started.append(copy)

        def came(m, i, ref):
            pltpu.make_async_copy(ref, ref, sems_in.at[m, i]).wait()

        halves = []
        for m in range(n):
            columns = full[m].shape[-1]
            halves.append(((0, columns // 2), (columns // 2, columns // 2)))
        order = range(n)
        for m in order:
            own = here[m % 3].at[m // 3]
            go(m, 0, own, piece(m, a, b), p.at(a + 1, b))
            go(m, 1, own, piece(m, a, b), p.at(a - 1, b))
            go(m, 8, own, piece(m, a, b), p.partner())
            local = pltpu.make_async_copy(own, piece(m, a, b), sems_here.at[3 + m])
            local.start()
        for m in order:
            pltpu.make_async_copy(here[m % 3].at[m // 3], piece(m, a, b), sems_here.at[3 + m]).wait()
            came(m, 0, piece(m, a - 1, b))
            go(m, 2, piece(m, a - 1, b, halves[m][0]), piece(m, a - 1, b, halves[m][0]), p.at(a + 1, b))
            go(m, 9, piece(m, a - 1, b), piece(m, a - 1, b), p.partner())
            came(m, 1, piece(m, a + 1, b))
            go(m, 3, piece(m, a + 1, b, halves[m][1]), piece(m, a + 1, b, halves[m][1]), p.at(a - 1, b))
            go(m, 10, piece(m, a + 1, b), piece(m, a + 1, b), p.partner())
        for m in order:
            came(m, 2, piece(m, a + 2, b, halves[m][0]))
            came(m, 3, piece(m, a + 2, b, halves[m][1]))
            go(m, 4, group(m, b), group(m, b), p.at(a, b + 1))
            go(m, 5, group(m, b), group(m, b), p.at(a, b - 1))
            go(m, 11, piece(m, a + 2, b), piece(m, a + 2, b), p.partner())
        for m in order:
            came(m, 4, group(m, b - 1))
            go(m, 6, group(m, b - 1, halves[m][0]), group(m, b - 1, halves[m][0]), p.at(a, b + 1))
            go(m, 12, group(m, b - 1), group(m, b - 1), p.partner())
            came(m, 5, group(m, b + 1))
            go(m, 7, group(m, b + 1, halves[m][1]), group(m, b + 1, halves[m][1]), p.at(a, b - 1))
            go(m, 13, group(m, b + 1), group(m, b + 1), p.partner())
        for m in order:
            came(m, 6, group(m, b + 2, halves[m][0]))
            came(m, 7, group(m, b + 2, halves[m][1]))
            go(m, 14, group(m, b + 2), group(m, b + 2), p.partner())
        for copy in started:
            copy.wait_send()
        for m in order:
            for i in (8, 9, 10, 11):
                came(m, i, piece(m, a, b))
            for i in (12, 13, 14):
                came(m, i, group(m, b))

    for core in range(2):
        pl.when(p.core == core)(functools.partial(run, core))


def gathered(weights):
    layers = weights[0].shape[0]
    shapes = [(4, 4, 2) + w.shape[1:] for _ in range(layers) for w in weights]
    any_space = pl.BlockSpec(memory_space=pl.ANY)
    out = pl.pallas_call(
        functools.partial(gather_kernel, layers),
        out_shape=[jax.ShapeDtypeStruct(shape, BF16) for shape in shapes],
        in_specs=[any_space] * 3,
        out_specs=[any_space] * len(shapes),
        scratch_shapes=[pltpu.VMEM(w.shape, BF16) for w in weights]
        + [
            pltpu.SemaphoreType.DMA((len(shapes), 15)),
            pltpu.SemaphoreType.DMA((len(shapes), 15)),
            pltpu.SemaphoreType.DMA((3 + len(shapes),)),
        ],
        compiler_params=pltpu.CompilerParams(collective_id=0, has_side_effects=True),
        name="gather",
    )(*weights)
    whole = [w.reshape(-1, w.shape[-1]) for w in out]
    return [dict(zip(NAMES, whole[3 * i : 3 * i + 3], strict=True)) for i in range(layers)]


class Sum:
    SCRATCH = 22

    @staticmethod
    def scratch(rows, columns):
        half = columns // 2

        def wide(*lead):
            return pltpu.VMEM((2, *lead, rows, columns), F32)

        def sent(*lead):
            return pltpu.VMEM((2, *lead, rows, columns), BF16)

        def part(*lead):
            return pltpu.VMEM((2, *lead, rows, half), BF16)

        return [
            sent(16, 2),
            sent(16),
            wide(4),
            wide(4),
            wide(4),
            sent(4),
            part(4),
            part(4),
            sent(4),
            sent(4),
            sent(4),
            sent(4),
            wide(),
            wide(),
            wide(),
            sent(),
            part(),
            part(),
            sent(),
            sent(),
            sent(),
            sent(),
            sent(4),
            pltpu.SemaphoreType.DMA((2, 12)),
            pltpu.SemaphoreType.DMA((2, 12)),
        ]

    def __init__(self, p, refs, total, emit):
        self.p, self.total, self.emit = p, total, emit
        (self.term, self.swapped, self.ca, self.cp, self.cm, self.x1, self.r1a, self.r1b, self.x2p, self.x2m, self.r2p, self.r2m) = refs[:12]
        (self.db, self.dp, self.dm, self.y1, self.r3a, self.r3b, self.y2p, self.y2m, self.r4p, self.r4m, self.rx) = refs[12:23]
        self.out_sem, self.in_sem = refs[23:25]
        self.half = self.term.shape[-1] // 2

    def copies(self, hop, k):
        p, h = self.p, self.half

        def one(i, src, dst, place):
            return send(src, dst, self.out_sem.at[k, i], self.in_sem.at[k, i], place)

        low, high = pl.ds(0, h), pl.ds(h, h)
        if hop == 0:
            return [one(0, self.term.at[k, :, 1 - p.core], self.swapped.at[k], p.partner())]
        if hop == 1:
            return [
                one(1, self.x1.at[k, :, :, low], self.r1a.at[k], p.at(p.a + 1, p.b)),
                one(2, self.x1.at[k, :, :, high], self.r1b.at[k], p.at(p.a - 1, p.b)),
            ]
        if hop == 2:
            return [
                one(3, self.x2p.at[k], self.r2p.at[k], p.at(p.a + 1, p.b)),
                one(4, self.x2m.at[k], self.r2m.at[k], p.at(p.a - 1, p.b)),
            ]
        if hop == 3:
            return [
                one(5, self.y1.at[k, :, low], self.r3a.at[k], p.at(p.a, p.b + 1)),
                one(6, self.y1.at[k, :, high], self.r3b.at[k], p.at(p.a, p.b - 1)),
            ]
        if hop == 4:
            return [
                one(7, self.y2p.at[k], self.r4p.at[k], p.at(p.a, p.b + 1)),
                one(8, self.y2m.at[k], self.r4m.at[k], p.at(p.a, p.b - 1)),
            ]
        return [one(8 + d, self.rx.at[k, p.x], self.rx.at[k, p.x], p.along_x(d)) for d in (1, 2, 3)]

    def add(self, hop, k, u):
        p, h = self.p, self.half

        def f(ref, *index):
            return ref[index].astype(F32)

        low, high = slice(0, h), slice(h, None)
        if hop == 1:
            for quarter, ref in ((p.a, self.ca), (p.a + 1, self.cp), (p.a - 1, self.cm), (p.a + 2, self.x1)):
                for b in range(4):
                    chip = p.chip(quarter, b)
                    ref[k, b] = (f(self.term, k, chip, p.core) + f(self.swapped, k, chip)).astype(ref.dtype)
        if hop == 2:
            for b in range(4):
                self.x2p[k, b, :, low] = (self.cp[k, b, :, low] + f(self.r1a, k, b)).astype(BF16)
                self.x2p[k, b, :, high] = self.cp[k, b, :, high].astype(BF16)
                self.x2m[k, b, :, low] = self.cm[k, b, :, low].astype(BF16)
                self.x2m[k, b, :, high] = (self.cm[k, b, :, high] + f(self.r1b, k, b)).astype(BF16)
        if hop == 3:
            for place, ref in ((p.b, self.db), (p.b + 1, self.dp), (p.b - 1, self.dm), (p.b + 2, self.y1)):
                b = place % 4
                ref[k] = (self.ca[k, b] + f(self.r2p, k, b) + f(self.r2m, k, b)).astype(ref.dtype)
        if hop == 4:
            self.y2p[k, :, low] = (self.dp[k, :, low] + f(self.r3a, k)).astype(BF16)
            self.y2p[k, :, high] = self.dp[k, :, high].astype(BF16)
            self.y2m[k, :, low] = self.dm[k, :, low].astype(BF16)
            self.y2m[k, :, high] = (self.dm[k, :, high] + f(self.r3b, k)).astype(BF16)
        if hop == 5:
            self.rx[k, p.x] = (self.db[k] + f(self.r4p, k) + f(self.r4m, k)).astype(BF16)
        if hop == 6:
            self.emit(u, ((f(self.rx, k, 0) + f(self.rx, k, 1)) + (f(self.rx, k, 2) + f(self.rx, k, 3))).astype(BF16))

    def hop(self, hop, u):
        k = u % 2
        if hop:
            for copy in self.copies(hop - 1, k):
                copy.wait()
        self.add(hop, k, u)
        if hop < HOPS:
            for copy in self.copies(hop, k):
                copy.start()

    def step(self, t, first=1):
        for hop in range(HOPS, first - 1, -1):
            u = t - hop
            pl.when((u >= 0) & (u < self.total))(functools.partial(self.hop, hop, u))


ROWS, COLUMNS = 64, 256


def sum_kernel(layers, ff_units, d_units, *refs):
    n = 3 * layers
    terms, out, scratch, load_sem = refs[:n], refs[n], refs[n + 1 : -1], refs[-1]
    p = Place()
    meet(p.neighbours())
    per = ff_units + d_units
    total = layers * per

    def emit(u, value):
        out[u] = value

    sums = Sum(p, scratch, total, emit)

    def loads(u, k):
        which = []
        for number in range(layers):
            gate, up, down = terms[3 * number : 3 * number + 3]

            def both(j, gate=gate, up=up):
                at = pl.ds(pl.multiple_of(j * COLUMNS, COLUMNS), COLUMNS)
                return [
                    pltpu.make_async_copy(ref.at[:, :, :, at], sums.term.at[k, :, :, pl.ds(32 * i, 32)], load_sem.at[i])
                    for i, ref in enumerate((gate, up))
                ]

            def rows(q, down=down):
                at = pl.ds(pl.multiple_of(16 * q - 8 * (q // (d_units - 1)), 8), 16)
                return [
                    pltpu.make_async_copy(down.at[:, :, at, pl.ds(256 * i, 256)], sums.term.at[k, :, :, pl.ds(16 * i, 16)], load_sem.at[i])
                    for i in range(4)
                ]

            which += [(number * per, ff_units, both), (number * per + ff_units, d_units, rows)]
        return which

    def body(t, _):
        sums.step(t)
        k = t % 2
        for start, count, made in loads(t, k):

            @pl.when((t >= start) & (t < start + count))
            def _(start=start, made=made):
                copies = made(t - start)
                for copy in copies:
                    copy.start()
                for copy in copies:
                    copy.wait()

        pl.when(t < total)(functools.partial(sums.hop, 0, t))

    lax.fori_loop(0, total + HOPS, lambda t, c: (body(t, c), c)[1], 0)


def summed(terms):
    layers = len(terms)
    flat = [t.reshape(16, 2, t.shape[0] // 32, t.shape[1]) for one in terms for t in one]
    d_rows = terms[0][2].shape[0] // 32
    ff_units, d_units = terms[0][0].shape[1] // COLUMNS, -(-d_rows // 16)
    per = ff_units + d_units
    out = pl.pallas_call(
        functools.partial(sum_kernel, layers, ff_units, d_units),
        out_shape=jax.ShapeDtypeStruct((layers * per, ROWS, COLUMNS), BF16),
        in_specs=[pl.BlockSpec(memory_space=pl.ANY)] * len(flat),
        out_specs=pl.BlockSpec(memory_space=pltpu.VMEM),
        scratch_shapes=Sum.scratch(ROWS, COLUMNS) + [pltpu.SemaphoreType.DMA((4,))],
        compiler_params=pltpu.CompilerParams(collective_id=1, has_side_effects=True, vmem_limit_bytes=48 * 2**20),
        name="sum",
    )(*flat)
    blocks = []
    for number in range(layers):
        one = out[number * per : (number + 1) * per]
        both = one[:ff_units].reshape(ff_units, 2, 32, COLUMNS).transpose(1, 2, 0, 3).reshape(2, 32, -1)
        down = one[ff_units:].reshape(d_units, 4, 16, COLUMNS).transpose(0, 2, 1, 3).reshape(d_units * 16, -1)
        kept = 16 * (d_units - 1)
        down = jnp.concatenate([down[: kept - (16 * d_units - d_rows)], down[kept:]]) if 16 * d_units != d_rows else down
        blocks.append([both[0], both[1], down])
    return blocks


def solution(mesh):
    def step(x, dy, *arrays):
        weights, m, v = (arrays[i : i + 3] for i in (0, 3, 6))
        layers = weights[0].shape[0]
        whole = gathered(weights)
        h, kept = x[0], []
        for number in range(layers):
            kept.append(h)
            h = layer(h, whole[number])
        by_h, terms = dy[0], [None] * layers
        for number in reversed(range(layers)):
            _, back = jax.vjp(lambda w, h: layer(h, w), whole[number], kept[number])
            by_w, by_h = back(by_h)
            terms[number] = [by_w[name] for name in NAMES]
        mine = summed(terms)
        gradients = [jnp.stack([mine[number][i] for number in range(layers)]).astype(jnp.float32) for i in range(3)]
        new = [adamw(w.astype(jnp.float32), m, v, g) for w, m, v, g in zip(weights, m, v, gradients, strict=True)]
        return tuple(one[which] for which in range(3) for one in new)

    states, cut = P(("rep", "r", "s"), None, None), P(None, "s", None)
    return jax.shard_map(
        step,
        mesh=mesh,
        in_specs=(states, states) + (cut,) * 9,
        out_specs=(P("rep", "s", None),) * 9,
        check_vma=False,
    )
```

time: 1040 us -> 768 us (0.74)
  waiting for transfers between devices: 605 us -> 0 us
  Pallas kernels: 0 us -> 350 us
  between operations: 14.5 us -> 1.37 us
    reduce_scatter x6 -> x0, waiting for transfers between devices: 386 us -> none  [summed(): lax.psum_scatter(term, 's', scatter_dimension=0, tiled=True)]
    pallas_call x0 -> x2, Pallas kernels: none -> 350 us  [the longest x1 234 us: summed(): pl.pallas_call(functools.partial(sum_kernel, layers, ff_units, d_units),...]
    all_gather x6 -> x0, waiting for transfers between devices: 168 us -> none  [fetched(): lax.all_gather(w[number], 's', axis=0, tiled=True)]
    psum x1 -> x0, waiting for transfers between devices: 49.6 us -> none  [summed(): lax.psum(lax.psum_scatter(term, 's', scatter_dimension=0, tiled=True), 'r')]
  transfers between devices with their start and end apart: 13 -> 0, of which waited for: 12 -> 0; matrix products, arithmetic and copies ran while one was open for 28% -> 0% of each run, Pallas kernels for 0% -> 0%
where the time goes in v1:
time: 768 us; the launch traced here: 758 us
  matrix products  374 us (49%)
  Pallas kernels  350 us (46%)
  other arithmetic  17 us (2%)
  local copies, waits for them, and re-layouts  16.2 us (2%)
    pallas_call x1, Pallas kernels, summed(): pl.pallas_call(functools.partial(sum_kernel, layers, ff_units, d_units),...  234 us
    dot_general x5, matrix products, layer(): gate = jnp.dot(a, w['w_gate'], preferred_element_type=jnp.float32)  134 us
    dot_general x5, matrix products, layer(): up = jnp.dot(a, w['w_up'], preferred_element_type=jnp.float32)  127 us
    pallas_call x1, Pallas kernels, gathered(): pl.pallas_call(functools.partial(gather_kernel, layers), out_shape=[jax.S...  116 us
    dot_general x5, matrix products, matmul(): jnp.dot(a, w, preferred_element_type=jnp.float32).astype(jnp.bfloat16)  113 us

profile of v1, /device:TPU:0, one launch (start us, length us, event | category | flops | bytes accessed | tf_op | source)
XLA Modules:
  0.0 758.3 jit_solution(12478521996242520993)
XLA Ops:
  0.6 116.2 %gather.1 = (bf16[4,4,2,32,3328]{4,3,2,1,0:T(8,128)(2,1)}, bf16[4,4,2,32,3328]{4,3,2,1,0:T(8,128)(2,1)}, bf16[4,4,2,104,1024]{4,3,2,1,0:T(8,128)(2,1)}, bf16[4,4...) custom-call(bf16[2,32,3328]{2,1,0:T(8,128)(2,1)} %refs_0_.1, ...), custom_call_target="tpu_custom_call" | custom-call | tf_op jit(solution)/shard_map/gather/pallas_call | solution.py:164
  116.8 6.6 copy.31
  123.4 3.1 fusion.15
  126.5 0.0 copy-start.12
  126.5 22.1 %fusion.43 = f32[2048,3328]{1,0:T(8,128)} fusion(bf16[1024,3328]{1,0:T(8,128)(2,1)} %bitcast.116, bf16[1,2048,1024]{2,1,0:T(8,128)(2,1)} %param.11, f32[2048]{0:T(1024)S(1)} %add_rsqrt_fusion), kind=kOutput, calls=%fused_computation.56 | convolution fusion | flops 13964935168 | bytes 38281216 | tf_op jit(solution)/shard_map/dot_general | solution.py:28
  148.5 0.0 copy-done.12
  148.5 32.7 %multiply_convert_fusion.1 = (bf16[2048,3328]{1,0:T(8,128)(2,1)}, f32[2048,3328]{1,0:T(8,128)}) fusion(f32[2048,3328]{1,0:T(8,128)} %fusion.43, bf16[1024,3328]{1,0:T(8,128)(2,1)} %bitcast.115, bf16[1,2048,1024]{2,1,0:T(8,128)(2,1)} %param.11, f32[2048]{0:T(1024)S(1)} %add_rsqrt_fusion), kind=kOutput, calls=%fused_computation.17 | convolution fusion | flops 14005829632 | bytes 79175680 | tf_op jit(solution)/shard_map/dot_general | solution.py:29
  181.2 22.3 %fusion.19 = (f32[2048]{0:T(1024)S(1)}, bf16[2048,1024]{0,1:T(8,128)(2,1)}) fusion(bf16[2048,3328]{1,0:T(8,128)(2,1)} %get-tuple-element.38, bf16[3328,1024]{1,0:T(8,128)(2,1)} %bitcast.108, bf16[1,2048,1024]{1,2,0:T(8,128)(2,1)} %copy.31), kind=kOutput, calls=%fused_computation.37 | convolution fusion | flops 13969127424 | bytes 28844032 | tf_op jit(solution)/shard_map/dot_general | solution.py:17
  203.5 0.0 copy-start.10
  203.5 0.0 copy-start
  203.5 21.4 %convolution_convert_fusion.1 = bf16[3328,2048]{0,1:T(8,128)(2,1)} fusion(bf16[3328,1024]{1,0:T(8,128)(2,1)} %bitcast.114, bf16[1,2048,1024]{2,1,0:T(8,128)(2,1)} %param.12), kind=kOutput, calls=%fused_computation.23 | convolution fusion | flops 13965459456 | bytes 24641536 | tf_op jit(solution)/shard_map/transpose(jvp())/dot_general | solution.py:17
  224.9 0.0 copy-done.10
  225.0 0.0 copy-done
  225.0 0.0 copy-start.8
  225.0 21.0 %fusion.37 = f32[2048,3328]{1,0:T(8,128)} fusion(bf16[1024,3328]{1,0:T(8,128)(2,1)} %bitcast.112, bf16[2048,1024]{0,1:T(8,128)(2,1)S(1)} %copy-done, f32[2048]{0:T(1024)S(1)} %fusion.60), kind=kOutput, calls=%fused_computation.53 | convolution fusion | flops 13964935168 | bytes 38281216 | tf_op jit(solution)/shard_map/jvp()/dot_general | solution.py:29
  245.9 39.8 %fusion.2 = (bf16[2048,3328]{1,0:T(8,128)(2,1)}, f32[2048,3328]{1,0:T(8,128)}) fusion(f32[2048,3328]{1,0:T(8,128)} %fusion.37, bf16[3328,2048]{0,1:T(8,128)(2,1)} %convolution_convert_fusion.1, bf16[1024,3328]{1,0:T(8,128)(2,1)} %bitcast.110, bf16[2048,1024]{0,1:T(8,128)(2,1)} %get-tuple-element.41, f32[2048]{0:T(1024)S(1)} %fusion.60), kind=kOutput, calls=%fused_computation.6 | convolution fusion | flops 14046724096 | bytes 92807168 | tf_op jit(solution)/shard_map/jvp()/dot_general | solution.py:28
  285.8 0.0 copy-start.1
  285.8 0.0 copy-start.14
  285.8 24.0 %fusion.12 = bf16[2048,1024]{0,1:T(8,128)(2,1)} fusion(bf16[1024,3328]{1,0:T(8,128)(2,1)} %bitcast.113, bf16[3328,2048]{0,1:T(8,128)(2,1)} %convolution_convert_fusion.1, f32[2048,3328]{1,0:T(8,128)} %get-tuple-element.43), kind=kOutput, calls=%fused_computation.21 | convolution fusion | flops 13999538176 | bytes 51904512 | tf_op jit(solution)/shard_map/transpose(jvp())/dot_general | solution.py:29
  309.8 0.0 copy-done.1
  309.8 0.0 copy-done.14
  309.8 19.9 %fusion.21 = (f32[2048]{0:T(1024)S(1)}, bf16[2048,1024]{0,1:T(8,128)(2,1)}) fusion(bf16[2048,1024]{0,1:T(8,128)(2,1)S(1)} %copy-done.1, bf16[2048,1024]{0,1:T(8,128)(2,1)} %fusion.12, bf16[2048,3328]{1,0:T(8,128)(2,1)} %get-tuple-element.42, bf16[1024,3328]{1,0:T(8,128)(2,1)S(1)} %bitcast.111), kind=kOutput, calls=%fused_computation.39 | convolution fusion | flops 13969127424 | bytes 33038336 | tf_op jit(solution)/shard_map/transpose(jvp())/dot_general | solution.py:28
  329.7 0.0 copy-start.11
  329.7 6.5 copy.32
  336.2 0.0 copy-done.11
  336.2 0.0 copy-done.8
  336.2 7.6 %fusion.30 = bf16[2048,1024]{0,1:T(8,128)(2,1)} fusion(bf16[2048,1024]{0,1:T(8,128)(2,1)} %get-tuple-element.41, bf16[2048,1024]{0,1:T(8,128)(2,1)} %get-tuple-element.45, bf16[1,2048,1024]{1,2,0:T(8,128)(2,1)} %copy.32, f32[2048]{0:T(1024)S(1)} %multiply_multiply_fusion.3, f32[2048]{0:T(1024)S(1)} %fusion.60), kind=kLoop, calls=%fused_computation.48 | loop fusion | flops 14680064 | bytes 16793600 | tf_op jit(solution)/shard_map/transpose(jvp())/add_any | solution.py:21
  343.9 0.0 copy-start.13
  343.9 21.3 %convolution_convert_fusion = bf16[2048,3328]{1,0:T(8,128)(2,1)} fusion(bf16[2048,1024]{0,1:T(8,128)(2,1)} %fusion.30, bf16[3328,1024]{1,0:T(8,128)(2,1)} %bitcast.109), kind=kOutput, calls=%fused_computation.22 | convolution fusion | flops 13965459456 | bytes 24641536 | tf_op jit(solution)/shard_map/transpose(jvp())/dot_general | solution.py:17
  365.1 0.0 copy-done.13
  365.1 31.4 %fusion.22 = bf16[1024,3328]{1,0:T(8,128)(2,1)} fusion(f32[2048,3328]{1,0:T(8,128)} %fusion.43, f32[2048,3328]{1,0:T(8,128)} %get-tuple-element.39, bf16[2048,3328]{1,0:T(8,128)(2,1)} %convolution_convert_fusion, bf16[1,2048,1024]{1,2,0:T(8,128)(2,1)} %copy.31, f32[2048]{0:T(1024)S(1)} %copy-done.13), kind=kOutput, calls=%fused_computation.41 | convolution fusion | flops 14043316224 | bytes 79175680 | tf_op jit(solution)/shard_map/transpose(jvp())/dot_general | solution.py:28
  396.5 25.3 %fusion.27 = bf16[1024,3328]{1,0:T(8,128)(2,1)} fusion(bf16[2048,3328]{1,0:T(8,128)(2,1)} %convolution_convert_fusion, f32[2048,3328]{1,0:T(8,128)} %fusion.43, bf16[1,2048,1024]{1,2,0:T(8,128)(2,1)} %copy.31, f32[2048]{0:T(1024)S(1)} %copy-done.13), kind=kOutput, calls=%fused_computation.44 | convolution fusion | flops 14009237504 | bytes 51912704 | tf_op jit(solution)/shard_map/transpose(jvp())/dot_general | solution.py:29
  421.8 0.0 copy-start.2
  421.8 0.0 copy-start.9
  421.8 20.8 %convolution_convert_fusion.3 = bf16[3328,1024]{1,0:T(8,128)(2,1)} fusion(bf16[2048,3328]{1,0:T(8,128)(2,1)} %get-tuple-element.38, bf16[2048,1024]{0,1:T(8,128)(2,1)} %fusion.30), kind=kOutput, calls=%fused_computation.46 | convolution fusion | flops 13962051584 | bytes 24641536 | tf_op jit(solution)/shard_map/transpose(jvp())/dot_general | solution.py:17
  442.6 0.0 copy-done.2
  442.6 0.0 copy-done.9
  442.6 20.4 %convolution_convert_fusion.2 = bf16[1024,3328]{1,0:T(8,128)(2,1)} fusion(bf16[2048,3328]{1,0:T(8,128)(2,1)} %get-tuple-element.42, bf16[2048,1024]{0,1:T(8,128)(2,1)S(1)} %copy-done.2, f32[2048]{0:T(1024)S(1)} %copy-done.9), kind=kOutput, calls=%fused_computation.45 | convolution fusion | flops 13964935168 | bytes 24649728 | tf_op jit(solution)/shard_map/transpose(jvp())/dot_general | solution.py:28
  463.1 24.3 %fusion.26 = bf16[1024,3328]{1,0:T(8,128)(2,1)} fusion(bf16[3328,2048]{0,1:T(8,128)(2,1)} %convolution_convert_fusion.1, bf16[2048,1024]{0,1:T(8,128)(2,1)S(1)} %copy-done.2, f32[2048]{0:T(1024)S(1)} %copy-done.9, f32[2048,3328]{1,0:T(8,128)} %get-tuple-element.43), kind=kOutput, calls=%fused_computation.43 | convolution fusion | flops 14009237504 | bytes 51912704 | tf_op jit(solution)/shard_map/transpose(jvp())/dot_general | solution.py:29
  487.3 27.2 %fusion.25 = bf16[3328,1024]{1,0:T(8,128)(2,1)} fusion(f32[2048,3328]{1,0:T(8,128)} %fusion.37, bf16[1,2048,1024]{2,1,0:T(8,128)(2,1)} %param.12, f32[2048,3328]{1,0:T(8,128)} %get-tuple-element.43), kind=kOutput, calls=%fused_computation.42 | convolution fusion | flops 14002946048 | bytes 65536000 | tf_op jit(solution)/shard_map/transpose(jvp())/dot_general | solution.py:17
  514.5 0.0 copy-start.4
  514.5 0.0 copy-start.5
  514.5 233.7 %sum.1 = bf16[40,64,256]{2,1,0:T(8,128)(2,1)S(1)} custom-call(bf16[16,2,32,3328]{3,2,1,0:T(8,128)(2,1)} %bitcast.86, bf16[16,2,32,3328]{3,2,1,0:T(8,128)(2,1)} %bitcast.87, bf16[16,2,104,1024]{3,2,1,0:T(8,128)(2,1)} %bitcast.88, bf16[16,2,32,3328]{3,2,1,0:T(8,128)(2,1)} %bitcast.89, bf16[16,2,32,3328]{3,2,1,0:T(8,128)(2,1)} %bitcast.90, ...), custom_call_target="tpu_custom_call" | custom-call | tf_op jit(solution)/shard_map/sum/pallas_call | solution.py:374
  748.2 0.1 fusion.73
  748.3 0.2 copy.47
  748.6 0.9 slice.65
  749.5 0.2 copy.48
  749.7 0.0 copy-start.3
  749.8 0.9 slice.62
  750.6 0.2 slice.69
  750.8 0.2 slice.67
  751.0 0.0 copy-done.4
  751.0 0.0 copy-done.5
  751.0 0.0 copy-start.6
  751.0 0.0 copy-start.7
  751.0 4.7 fusion.47
  755.8 0.1 copy.36
  756.0 0.1 copy.38
  756.2 0.0 copy-done.3
  756.2 0.0 copy-done.6
  756.2 0.0 copy-done.7
  756.3 1.6 fusion.55
  (17 shorter events, 0.3 us)
Async XLA Ops:
  126.5 22.1 %copy-start.12 = (f32[2048]{0:T(1024)}, f32[2048]{0:T(1024)S(1)}, u32[]{:S(2)}) copy-start(f32[2048]{0:T(1024)S(1)} %add_rsqrt_fusion) | copy-start | bytes 24580
  203.5 21.4 %copy-start.10 = (f32[2048]{0:T(1024)}, f32[2048]{0:T(1024)S(1)}, u32[]{:S(2)}) copy-start(f32[2048]{0:T(1024)S(1)} %get-tuple-element.40) | copy-start | bytes 24580
  203.5 21.5 %copy-start = (bf16[2048,1024]{0,1:T(8,128)(2,1)S(1)}, bf16[2048,1024]{0,1:T(8,128)(2,1)}, u32[]{:S(2)}) copy-start(bf16[2048,1024]{0,1:T(8,128)(2,1)} %get-tuple-element.41) | copy-start | bytes 12582916
  225.0 111.3 %copy-start.8 = (f32[2048]{0:T(1024)}, f32[2048]{0:T(1024)S(1)}, u32[]{:S(2)}) copy-start(f32[2048]{0:T(1024)S(1)} %fusion.60) | copy-start | bytes 24580
  285.8 24.0 %copy-start.1 = (bf16[2048,1024]{0,1:T(8,128)(2,1)S(1)}, bf16[2048,1024]{0,1:T(8,128)(2,1)}, u32[]{:S(2)}) copy-start(bf16[2048,1024]{0,1:T(8,128)(2,1)} %get-tuple-element.41) | copy-start | bytes 12582916
  285.8 24.0 %copy-start.14 = (bf16[4,4,2,32,3328]{4,3,2,1,0:T(8,128)(2,1)S(1)}, bf16[4,4,2,32,3328]{4,3,2,1,0:T(8,128)(2,1)}, u32[]{:S(2)}) copy-start(bf16[4,4,2,32,3328]{4,3,2,1,0:T(8,128)(2,1)} %get-tuple-element.18) | copy-start | bytes 20447236
  329.7 6.6 copy-start.11
  343.9 21.3 %copy-start.13 = (f32[2048]{0:T(1024)S(1)}, f32[2048]{0:T(1024)}, u32[]{:S(2)}) copy-start(f32[2048]{0:T(1024)} %copy-done.12) | copy-start | bytes 24580
  421.8 20.8 %copy-start.2 = (bf16[2048,1024]{0,1:T(8,128)(2,1)S(1)}, bf16[2048,1024]{0,1:T(8,128)(2,1)}, u32[]{:S(2)}) copy-start(bf16[2048,1024]{0,1:T(8,128)(2,1)} %get-tuple-element.41) | copy-start | bytes 12582916
  421.8 20.8 %copy-start.9 = (f32[2048]{0:T(1024)S(1)}, f32[2048]{0:T(1024)}, u32[]{:S(2)}) copy-start(f32[2048]{0:T(1024)} %copy-done.8) | copy-start | bytes 24580
  514.5 236.5 %copy-start.4 = (bf16[2,32,3328]{2,1,0:T(8,128)(2,1)S(1)}, bf16[2,32,3328]{2,1,0:T(8,128)(2,1)}, u32[]{:S(2)}) copy-start(bf16[2,32,3328]{2,1,0:T(8,128)(2,1)} %refs_0_.1) | copy-start | bytes 1277956
  514.5 236.5 %copy-start.5 = (bf16[2,32,3328]{2,1,0:T(8,128)(2,1)S(1)}, bf16[2,32,3328]{2,1,0:T(8,128)(2,1)}, u32[]{:S(2)}) copy-start(bf16[2,32,3328]{2,1,0:T(8,128)(2,1)} %refs_1_.1) | copy-start | bytes 1277956
  749.7 6.5 copy-start.3
  751.0 5.3 copy-start.6
  751.0 5.2 copy-start.7

commit v2 on v0

v2 whole, which is shorter than its diff:
```python
import functools

import jax
import jax.numpy as jnp
from jax import lax
from jax.experimental import pallas as pl
from jax.experimental.pallas import tpu as pltpu
from jax.sharding import PartitionSpec as P

NAMES = ("w_gate", "w_up", "w_down")
MESH = pl.DeviceIdType.MESH
F32, BF16 = jnp.float32, jnp.bfloat16
HOPS = 6
VMEM_LIMIT = 67043328
PLAIN, BY_COLUMNS, BY_ROWS = (((1,), (0,)), ((), ())), (((1,), (1,)), ((), ())), (((0,), (0,)), ((), ()))
HERE, NEXT, FAR, LAST = range(4)
TILE = 256


def adamw(w, m, v, g):
    m = 0.9 * m + 0.1 * g
    v = 0.95 * v + 0.05 * g * g
    step = m * lax.rsqrt(v + 1e-8) + 0.1 * w
    return (w - 0.02 * step).astype(jnp.bfloat16), m, v


def dot(a, b, dims=PLAIN):
    return lax.dot_general(a, b, dims, preferred_element_type=F32)


def block(n, size=TILE):
    return pl.ds(pl.multiple_of(n * size, size), size)


def added(values):
    total = None
    for value in values:
        total = value if total is None else total + value
    return total


RING, OTHERS = ((NEXT, HERE), (LAST, HERE), (HERE, NEXT), (HERE, LAST)), (NEXT, FAR, LAST)


class Place:
    def __init__(self):
        self.s, self.x = lax.axis_index("s"), lax.axis_index("r")
        self.core = lax.rem(self.s, 2)
        y, z = lax.div(self.s, 8), lax.rem(lax.div(self.s, 2), 4)
        a = y * (1 - self.core) + z * self.core
        b = z * (1 - self.core) + y * self.core
        step_a, step_b = 4 - 3 * self.core, 1 + 3 * self.core
        self.a, self.b = [[lax.rem(at + d, 4) for d in range(4)] for at in (a, b)]
        self.chips = [[self.a[d] * step_a + self.b[e] * step_b for e in range(4)] for d in range(4)]
        self.devices = {(d, e): 2 * self.chips[d][e] + self.core for d in range(4) for e in range(4)}
        self.across = self.s + 1 - 2 * self.core
        self.xs = [lax.rem(self.x + d, 4) for d in range(4)]

    def at(self, d, e):
        return {"s": self.devices[d, e]}

    def partner(self):
        return {"s": self.across}

    def along_x(self, d):
        return {"r": self.xs[d]}

    def neighbours(self):
        return [self.partner()] + [self.at(*there) for there in RING] + [self.along_x(d) for d in OTHERS]


def meet(places):
    barrier = pltpu.get_barrier_semaphore()
    for place in places:
        pl.semaphore_signal(barrier, inc=1, device_id=place, device_id_type=MESH)
    pl.semaphore_wait(barrier, len(places))


def send(src, dst, send_sem, recv_sem, place):
    return pltpu.make_async_remote_copy(src_ref=src, dst_ref=dst, send_sem=send_sem, recv_sem=recv_sem, device_id=place, device_id_type=MESH)


class Gather:
    SLOTS = 12

    def __init__(self, p, n, m, here, full, sems):
        self.p, self.n, self.m, self.here, self.full = p, n, m, here, full
        self.out_sem, self.in_sem, self.here_sem, self.own_sem = sems
        self.total = 2 * (n + m)

    def hop(self, core, kind, hop, u, later):
        p, k = self.p, lax.rem(u, self.SLOTS)
        at = u - self.m * later if kind == 0 else u - self.n * (1 + later)
        here = self.here[kind].at[at]
        rows = here.shape[0]
        f = self.full[kind].at[at]
        cut = (rows // 2 + 7) // 8 * 8
        low, high = (0, cut), (cut, rows - cut)

        def piece(d, e, half=(0, rows)):
            if kind:
                return f.at[pl.ds(pl.multiple_of(rows * p.devices[d, e], 8) + half[0], half[1])]
            whole = f.at[p.a[d], p.b[e], core] if core == 0 else f.at[p.b[e], p.a[d], core]
            return whole.at[pl.ds(*half)]

        def group(e, half=(0, rows)):
            if kind:
                return [piece(d, e, half) for d in range(4)]
            whole = f.at[:, p.b[e], core] if core == 0 else f.at[p.b[e], :, core]
            return [whole.at[:, pl.ds(*half)]]

        def of_size(lines, columns, half=(0, rows)):
            if kind:
                return f.at[pl.ds(0, lines * columns * half[1])]
            return f.at[pl.ds(0, lines), pl.ds(0, columns), 0, pl.ds(*half)]

        def go(i, ref, place, left=0, src=None):
            send(ref if src is None else src, ref, self.out_sem.at[k, left], self.in_sem.at[k, i], place).start()

        def over(ref, src=None):
            go(8, ref, p.partner(), FAR, src)

        def came(sem, ref):
            pltpu.make_async_copy(ref, ref, sem).wait()

        def all_came(i, columns, half=(0, rows)):
            came(self.in_sem.at[k, i], of_size(1, columns, half))

        if hop == 0:
            came(self.here_sem.at[u], here)
            own = piece(HERE, HERE)
            go(0, own, p.at(NEXT, HERE), src=here)
            go(1, own, p.at(LAST, HERE), src=here)
            over(own, src=here)
            pltpu.make_async_copy(here, own, self.own_sem.at[k]).start()
        if hop == 1:
            all_came(0, 1)
            go(2, piece(LAST, HERE, low), p.at(NEXT, HERE))
            over(piece(LAST, HERE))
            all_came(1, 1)
            go(3, piece(NEXT, HERE, high), p.at(LAST, HERE))
            over(piece(NEXT, HERE))
        if hop == 2:
            came(self.own_sem.at[k], piece(HERE, HERE))
            all_came(2, 1, low)
            all_came(3, 1, high)
            for one in group(HERE):
                go(4, one, p.at(HERE, NEXT), 1)
                go(5, one, p.at(HERE, LAST), 1)
            over(piece(FAR, HERE))
        if hop == 3:
            all_came(4, 4)
            for one in group(LAST, low):
                go(6, one, p.at(HERE, NEXT), 1)
            for one in group(LAST):
                over(one)
            all_came(5, 4)
            for one in group(NEXT, high):
                go(7, one, p.at(HERE, LAST), 1)
            for one in group(NEXT):
                over(one)
        if hop == 4:
            all_came(6, 4, low)
            all_came(7, 4, high)
            for one in group(FAR):
                over(one)
        if hop == 5:
            came(self.in_sem.at[k, 8], of_size(4, 4))
            for i, (lines, columns) in enumerate(((1, 3), (3, 4), (4, 4))):
                came(self.out_sem.at[k, i], of_size(lines, columns))

    def step(self, t):
        def both(core, hop, u):
            later = lax.div(u, self.n + self.m)
            is_down = u - (self.n + self.m) * later >= self.n
            pl.when(~is_down)(lambda: self.hop(core, 0, hop, u, later))
            pl.when(is_down)(lambda: self.hop(core, 1, hop, u, later))

        def run(core):
            for hop in range(5, -1, -1):
                u = t - 2 * hop
                pl.when((u >= 0) & (u < self.total))(functools.partial(both, core, hop, u))

        for core in (0, 1):
            pl.when(self.p.core == core)(functools.partial(run, core))

    def steps(self, first, count):
        lax.fori_loop(0, count, lambda i, c: (self.step(first + i), c)[1], 0)


def normed(wide):
    return (wide * lax.rsqrt(jnp.mean(wide * wide, -1, keepdims=True) + 1e-6)).astype(BF16)


def forward_kernel(x, dy, w_gate, w_up, w_down, gu, d, pq, act_out, at_out, h_out, dw_out,
                   a, dyv, act, wt, wdt, pqs, h, ats, xs, dws, here_gu, here_d, out_sem, in_sem, here_sem, own_sem,
                   x_sem, dy_sem, act_sem, h_sem, w_sem, wd_sem, pq_sem, at_sem, xs_sem, dw_sem):
    tokens, width = a.shape
    n, m = act.shape[0], h.shape[0]
    p = Place()
    gather = Gather(p, n, m, (here_gu, here_d), (gu, d), (out_sem, in_sem, here_sem, own_sem))
    copy = pltpu.make_async_copy
    copy(x, a, x_sem).start()
    for layer in range(2):

        def bring(j, c, layer=layer):
            u = j + layer * (n + m)
            copy(w_gate.at[layer, :, block(j)], here_gu.at[layer * n + j, pl.ds(0, 32)], here_sem.at[u]).start()
            copy(w_up.at[layer, :, block(j)], here_gu.at[layer * n + j, pl.ds(32, 32)], here_sem.at[u]).start()
            return c

        lax.fori_loop(0, n, bring, 0)
        for i in range(m):
            u = n + i + layer * (n + m)
            copy(w_down.at[layer, :, pl.ds(i * TILE, TILE)], here_d.at[layer * m + i], here_sem.at[u]).start()
    copy(dy, dyv, dy_sem).start()
    meet(p.neighbours()[:5])

    def transposed(layer, i):
        return copy(ats.at[lax.rem(i, 2)], at_out.at[layer, :, block(i)], at_sem.at[lax.rem(i, 2)])

    def norm(layer, i, wide):
        value = normed(wide)
        a[block(i)] = value
        pl.when(i >= 2)(lambda: transposed(layer, i - 2).wait())
        ats[lax.rem(i, 2)] = value.T
        transposed(layer, i).start()

    def norm_done(layer):
        for i in (tokens // TILE - 2, tokens // TILE - 1):
            transposed(layer, i).wait()

    def start(t, c):
        gather.step(t)

        @pl.when(t == 2)
        def _():
            copy(x, a, x_sem).wait()

        @pl.when((t >= 2) & (t < 2 + tokens // TILE))
        def _():
            norm(0, t - 2, a[block(t - 2)].astype(F32))

        return c

    lax.fori_loop(0, 11, start, 0)
    norm_done(0)

    def w_tile(unit, k):
        return copy(gu.at[unit], wt.at[k], w_sem.at[k])

    def wd_tile(i, k):
        return copy(d.at[i], wdt.at[k], wd_sem.at[k])

    def x_tile(i, k):
        return copy(x.at[:, block(i)], xs.at[k], xs_sem.at[k])

    def pq_tile(layer, j, k):
        return copy(pqs.at[k], pq.at[layer * n + j], pq_sem.at[k])

    def dw_tile(j, k):
        return copy(dws.at[k], dw_out.at[block(j)], dw_sem.at[k])

    def act_tile(j):
        return copy(act.at[j], act_out.at[j], act_sem)

    base = 12 + n + m - 1

    def hidden(layer):
        def body(j, c):
            k = lax.rem(j, 2)
            if layer:

                def more(i, c):
                    pl.when((i == 0) | (lax.rem(j, 3) == 2))(lambda: gather.step(base + j + lax.div(j, 3) + i))
                    return c

                lax.fori_loop(0, 2, more, 0)
            else:
                gather.step(11 + j)

            @pl.when(j < n - 1)
            def _():
                w_tile(layer * n + j + 1, 1 - k).start()

            if layer == 0:

                @pl.when(j == n - 1)
                def _():
                    wd_tile(0, 0).start()
                    x_tile(0, 0).start()

            w_tile(layer * n + j, k).wait()
            pl.when(j >= 2)(lambda: pq_tile(layer, j - 2, k).wait())
            if layer:
                pl.when(j >= 2)(lambda: dw_tile(j - 2, k).wait())
            gate_w, up_w = (wt[k, :, :, :, 32 * i : 32 * i + 32, :].reshape(width, TILE) for i in (0, 1))
            for i in range(tokens // 512):
                rows = pl.ds(512 * i, 512)
                gate, up = dot(a[rows], gate_w), dot(a[rows], up_w)
                s = 0.5 * jnp.tanh(0.5 * gate) + 0.5
                silu = gate * s
                pqs[k, 0, rows] = silu
                pqs[k, 1, rows] = up * (s + silu * (1 - s))
                act[j, rows] = (silu * up).astype(BF16)
            if layer:
                dws[k] = dot(act[j], dyv[...], BY_ROWS).astype(BF16)
                dw_tile(j, k).start()
            else:
                act_tile(j).start()
            pq_tile(layer, j, k).start()
            return c

        lax.fori_loop(0, n, body, 0)
        for j in (n - 2, n - 1):
            pq_tile(layer, j, j % 2).wait()
            if layer:
                dw_tile(j, j % 2).wait()

    w_tile(0, 0).start()
    hidden(0)

    def h_tile(i):
        return copy(h.at[i], h_out.at[:, block(i)], h_sem)

    def down(i, c):
        k = lax.rem(i, 2)
        gather.step(11 + n + i)

        @pl.when(i < m - 1)
        def _():
            wd_tile(i + 1, 1 - k).start()
            x_tile(i + 1, 1 - k).start()

        @pl.when(i == m - 1)
        def _():
            w_tile(n, 0).start()

        wd_tile(i, k).wait()
        x_tile(i, k).wait()
        for r in range(tokens // 512):
            rows = pl.ds(512 * r, 512)
            out = added(dot(act[j, rows], wdt[k, pl.ds(TILE * j, TILE)]) for j in range(n))
            h[i, rows] = xs[k, rows] + out.astype(BF16)
        h_tile(i).start()
        return c

    lax.fori_loop(0, m, down, 0)

    def norm_later(i, c):
        norm(1, i, jnp.concatenate([h[q, block(i)] for q in range(m)], -1).astype(F32))
        return c

    lax.fori_loop(0, tokens // TILE, norm_later, 0)
    norm_done(1)
    copy(act, act_out, act_sem).wait()
    copy(dy, dyv, dy_sem).wait()
    hidden(1)
    gather.steps(base + n + n // 3, max(0, 2 * (n + m) + 10 - (base + n + n // 3)))
    copy(h, h, h_sem).wait()


def forward(x, dy, weights):
    tokens, width = x.shape
    w_gate, w_up, w_down = weights
    hidden, rows = w_gate.shape[-1], w_down.shape[1]
    n, m = hidden // TILE, width // TILE
    layers, pieces = 2, (4, 4, 2, 64, TILE)
    shapes = [
        ((layers * n, *pieces), BF16),
        ((layers * m, hidden, TILE), BF16),
        ((layers * n, 2, tokens, TILE), F32),
        ((n, tokens, TILE), BF16),
        ((layers, width, tokens), BF16),
        ((tokens, width), BF16),
        ((hidden, width), BF16),
    ]

    def twice(*shape, dtype=BF16):
        return pltpu.VMEM((2, *shape), dtype)

    def sems(*shape):
        return pltpu.SemaphoreType.DMA(shape)

    scratch = [
        pltpu.VMEM((tokens, width), BF16),
        pltpu.VMEM((tokens, width), BF16),
        pltpu.VMEM((n, tokens, TILE), BF16),
        twice(*pieces),
        twice(hidden, TILE),
        twice(2, tokens, TILE, dtype=F32),
        pltpu.VMEM((m, tokens, TILE), BF16),
        twice(width, TILE),
        twice(tokens, TILE),
        twice(TILE, width),
        pltpu.VMEM((layers * n, *pieces[3:]), BF16),
        pltpu.VMEM((layers * m, rows, TILE), BF16),
        sems(Gather.SLOTS, 3),
        sems(Gather.SLOTS, 9),
        sems(layers * (n + m)),
        sems(Gather.SLOTS),
    ]
    scratch += [sems() for _ in range(4)] + [sems(2) for _ in range(6)]
    return pl.pallas_call(
        forward_kernel,
        out_shape=[jax.ShapeDtypeStruct(*shape) for shape in shapes],
        in_specs=[pl.BlockSpec(memory_space=pl.ANY)] * 5,
        out_specs=[pl.BlockSpec(memory_space=pl.ANY)] * len(shapes),
        scratch_shapes=scratch,
        compiler_params=pltpu.CompilerParams(collective_id=0, has_side_effects=True, vmem_limit_bytes=VMEM_LIMIT),
        name="forward",
    )(x, dy, w_gate, w_up, w_down)


class Sum:
    @staticmethod
    def scratch(rows, columns):
        half = columns // 2

        def wide(*lead):
            return pltpu.VMEM((2, *lead, rows, columns), F32)

        def sent(*lead):
            return pltpu.VMEM((2, *lead, rows, columns), BF16)

        def part(*lead):
            return pltpu.VMEM((2, *lead, rows, half), BF16)

        return [
            sent(16, 2),
            sent(16),
            wide(4),
            wide(4),
            wide(4),
            sent(4),
            part(4),
            part(4),
            sent(4),
            sent(4),
            sent(4),
            sent(4),
            wide(),
            wide(),
            wide(),
            sent(),
            part(),
            part(),
            sent(),
            sent(),
            sent(),
            sent(),
            sent(4),
            pltpu.SemaphoreType.DMA((2, 12)),
            pltpu.SemaphoreType.DMA((2, 12)),
        ]

    def __init__(self, p, refs, emit):
        self.p, self.emit = p, emit
        (self.term, self.swapped, self.ca, self.cp, self.cm, self.x1, self.r1a, self.r1b, self.x2p, self.x2m, self.r2p, self.r2m) = refs[:12]
        (self.db, self.dp, self.dm, self.y1, self.r3a, self.r3b, self.y2p, self.y2m, self.r4p, self.r4m, self.rx) = refs[12:23]
        self.out_sem, self.in_sem = refs[23:25]
        self.half = self.term.shape[-1] // 2

    def copies(self, hop, k):
        p, h = self.p, self.half

        def one(i, src, dst, place):
            return send(src, dst, self.out_sem.at[k, i], self.in_sem.at[k, i], place)

        low, high = pl.ds(0, h), pl.ds(h, h)
        if hop == 0:
            return [one(0, self.term.at[k, :, 1 - p.core], self.swapped.at[k], p.partner())]
        if hop == 1:
            return [
                one(1, self.x1.at[k, :, :, low], self.r1a.at[k], p.at(NEXT, HERE)),
                one(2, self.x1.at[k, :, :, high], self.r1b.at[k], p.at(LAST, HERE)),
            ]
        if hop == 2:
            return [
                one(3, self.x2p.at[k], self.r2p.at[k], p.at(NEXT, HERE)),
                one(4, self.x2m.at[k], self.r2m.at[k], p.at(LAST, HERE)),
            ]
        if hop == 3:
            return [
                one(5, self.y1.at[k, :, low], self.r3a.at[k], p.at(HERE, NEXT)),
                one(6, self.y1.at[k, :, high], self.r3b.at[k], p.at(HERE, LAST)),
            ]
        if hop == 4:
            return [
                one(7, self.y2p.at[k], self.r4p.at[k], p.at(HERE, NEXT)),
                one(8, self.y2m.at[k], self.r4m.at[k], p.at(HERE, LAST)),
            ]
        return [one(8 + d, self.rx.at[k, p.x], self.rx.at[k, p.x], p.along_x(d)) for d in OTHERS]

    def add(self, hop, k, u):
        p, h = self.p, self.half

        def f(ref, *index):
            return ref[index].astype(F32)

        low, high = slice(0, h), slice(h, None)
        if hop == 1:
            for d, ref in enumerate((self.ca, self.cp, self.x1, self.cm)):
                for e in range(4):
                    chip = p.chips[d][e]
                    ref[k, e] = (f(self.term, k, chip, p.core) + f(self.swapped, k, chip)).astype(ref.dtype)
        if hop == 2:
            for b in range(4):
                self.x2p[k, b, :, low] = (self.cp[k, b, :, low] + f(self.r1a, k, b)).astype(BF16)
                self.x2p[k, b, :, high] = self.cp[k, b, :, high].astype(BF16)
                self.x2m[k, b, :, low] = self.cm[k, b, :, low].astype(BF16)
                self.x2m[k, b, :, high] = (self.cm[k, b, :, high] + f(self.r1b, k, b)).astype(BF16)
        if hop == 3:
            for e, ref in enumerate((self.db, self.dp, self.y1, self.dm)):
                ref[k] = (self.ca[k, e] + f(self.r2p, k, e) + f(self.r2m, k, e)).astype(ref.dtype)
        if hop == 4:
            self.y2p[k, :, low] = (self.dp[k, :, low] + f(self.r3a, k)).astype(BF16)
            self.y2p[k, :, high] = self.dp[k, :, high].astype(BF16)
            self.y2m[k, :, low] = self.dm[k, :, low].astype(BF16)
            self.y2m[k, :, high] = (self.dm[k, :, high] + f(self.r3b, k)).astype(BF16)
        if hop == 5:
            self.rx[k, p.x] = (self.db[k] + f(self.r4p, k) + f(self.r4m, k)).astype(BF16)
        if hop == 6:
            self.emit(u, ((f(self.rx, k, 0) + f(self.rx, k, 1)) + (f(self.rx, k, 2) + f(self.rx, k, 3))).astype(BF16))

    def hop(self, hop, u):
        k = lax.rem(u, 2)
        if hop:
            for copy in self.copies(hop - 1, k):
                copy.wait()
        self.add(hop, k, u)
        if hop < HOPS:
            for copy in self.copies(hop, k):
                copy.start()

    def step(self, t, first, last):
        for hop in range(HOPS, 0, -1):
            u = t - hop
            pl.when((u >= first) & (u < last))(functools.partial(self.hop, hop, u))


def backward_kernel(dy, gu, d, pq, act, at, h, dw1, g_gu, g_d, dgu_out, dw0, dh, av, dwt, load_sem, dh_sem, at_sem, gu_sem, wd_sem, pq_sem, act_sem, dgu_sem, dw_sem, dgc_sem, h_sem, *scratch):
    tokens, width = dh.shape
    n, q = g_gu.shape[0] // 2, g_d.shape[0] // 2
    half = len(scratch) // 2
    copy = pltpu.make_async_copy
    p = Place()
    overlap = 16 * q - dw1.shape[0] // 32

    def keep(out):
        def emit(u, value):
            out[u] = value

        return emit

    sum_gu, sum_d = Sum(p, scratch[:half], keep(g_gu)), Sum(p, scratch[half:], keep(g_d))
    copy(dy, dh, dh_sem).start()
    copy(at.at[1], av, at_sem).start()

    d_rows = dw1.shape[0] // 32

    def d_start(term, s, u):
        def one(i, c):
            rows = pl.ds(pl.multiple_of(d_rows * i + 16 * s - overlap * lax.div(s, q - 1), 8), 16)
            copy(term.at[rows], sum_d.term.at[lax.rem(u, 2), lax.div(i, 2), lax.rem(i, 2)], load_sem).start()
            return c

        lax.fori_loop(0, 32, one, 0)

    def d_step(term, s, first):
        sum_d.step(first + s, first, first + q)

        @pl.when(s < q)
        def _():
            whole = sum_d.term.at[lax.rem(first + s, 2)]
            copy(whole, whole, load_sem).wait()
            sum_d.hop(0, first + s)

        pl.when(s + 1 < q)(lambda: d_start(term, s + 1, first + s + 1))

    def gradients(layer, term, first, d_first):
        def phase(wdt, pqt, dgu):
            m = width // TILE

            def tiles(j, k):
                return [
                    copy(d.at[pl.ds(layer * m, m), block(j)], wdt.at[k], wd_sem.at[k]),
                    copy(pq.at[layer * n + j], pqt.at[k], pq_sem.at[k]),
                ]

            def dgu_tile(j, k):
                return copy(dgu.at[k], dgu_out.at[j], dgu_sem.at[k])

            def body(j, c):
                k = lax.rem(j, 2)
                sum_gu.step(first + j, first, first + n)
                pl.when(k == 0)(lambda: d_step(term, lax.div(j, 2), d_first))

                @pl.when(j < n - 1)
                def _():
                    for one in tiles(j + 1, 1 - k):
                        one.start()

                for one in tiles(j, k):
                    one.wait()
                if layer:
                    pl.when(j >= 2)(lambda: dgu_tile(j - 2, k).wait())
                for i in range(tokens // 512):
                    rows = pl.ds(512 * i, 512)
                    by_act = added(dot(dh[rows, TILE * e : TILE * e + TILE], wdt[k, e], BY_COLUMNS) for e in range(m))
                    by_act = by_act.astype(BF16).astype(F32)
                    dgu[k, 0, rows] = (by_act * pqt[k, 1, rows]).astype(BF16)
                    dgu[k, 1, rows] = (by_act * pqt[k, 0, rows]).astype(BF16)
                slot = lax.rem(first + j, 2)
                for i in range(m):
                    for e in (0, 1):
                        value = dot(av[TILE * i : TILE * i + TILE], dgu[k, e]).astype(BF16)
                        sum_gu.term[slot, 4 * i : 4 * i + 4, :, 32 * e : 32 * e + 32, :] = value.reshape(4, 2, 32, TILE)
                if layer:
                    dgu_tile(j, k).start()
                sum_gu.hop(0, first + j)
                return c

            for one in tiles(0, 0):
                one.start()
            lax.fori_loop(0, n, body, 0)
            if layer:
                for j in (n - 2, n - 1):
                    dgu_tile(j, j % 2).wait()

        pl.run_scoped(
            phase,
            pltpu.VMEM((2, width // TILE, TILE, TILE), BF16),
            pltpu.VMEM((2, 2, tokens, TILE), F32),
            pltpu.VMEM((2, 2, tokens, TILE), BF16),
        )

    def to_states(wv, dgc, hv):
        def rows_in(i, k):
            return [
                copy(dgu_out.at[:, :, block(i)], dgc.at[k], dgc_sem.at[k]),
                copy(h.at[block(i)], hv.at[k], h_sem.at[k]),
            ]

        def body(i, c):
            k = lax.rem(i, 2)
            sum_gu.step(n + i, 0, n)
            d_step(dw1, (n + 1) // 2 + i, 0)

            @pl.when(i < tokens // TILE - 1)
            def _():
                for one in rows_in(i + 1, 1 - k):
                    one.start()

            for one in rows_in(i, k):
                one.wait()
            parts = []
            for e in range(width // TILE):
                two = [
                    added(dot(dgc[k, j, o], wv[j, e, :, :, 32 * o : 32 * o + 32, :].reshape(TILE, TILE), BY_COLUMNS) for j in range(n))
                    for o in (0, 1)
                ]
                parts.append((two[0].astype(BF16) + two[1].astype(BF16)).astype(F32))
            by_a = jnp.concatenate(parts, -1)
            wide = hv[k].astype(F32)
            scale = lax.rsqrt(jnp.mean(wide * wide, -1, keepdims=True) + 1e-6)
            along = jnp.mean(by_a * wide, -1, keepdims=True)
            by_h = by_a * scale - wide * (scale * scale * scale * along)
            dh[block(i)] = dh[block(i)] + by_h.astype(BF16)
            return c

        for one in rows_in(0, 0):
            one.start()
        copy(gu.at[pl.ds(n, n)], wv, gu_sem).start()
        copy(gu.at[pl.ds(n, n)], wv, gu_sem).wait()
        lax.fori_loop(0, tokens // TILE, body, 0)

    def down(acts):
        def tile(j, k):
            return copy(act.at[j], acts.at[k], act_sem.at[k])

        def out(j, k):
            return copy(dwt.at[k], dw0.at[block(j)], dw_sem.at[k])

        def body(j, c):
            k = lax.rem(j, 2)
            pl.when(j < n - 1)(lambda: tile(j + 1, 1 - k).start())
            tile(j, k).wait()
            pl.when(j >= 2)(lambda: out(j - 2, k).wait())
            dwt[k] = dot(acts[k], dh[...], BY_ROWS).astype(BF16)
            out(j, k).start()
            return c

        tile(0, 0).start()
        lax.fori_loop(0, n, body, 0)
        for j in (n - 2, n - 1):
            out(j, j % 2).wait()

    d_start(dw1, 0, 0)
    meet(p.neighbours())
    copy(dy, dh, dh_sem).wait()
    copy(at.at[1], av, at_sem).wait()
    gradients(1, dw1, 0, 0)
    copy(at.at[0], av, at_sem).start()
    pl.run_scoped(
        to_states,
        pltpu.VMEM((n, 4, 4, 2, 64, TILE), BF16),
        pltpu.VMEM((2, n, 2, TILE, TILE), BF16),
        pltpu.VMEM((2, TILE, width), BF16),
    )
    pl.run_scoped(down, pltpu.VMEM((2, tokens, TILE), BF16))
    d_start(dw0, 0, q)
    copy(at.at[0], av, at_sem).wait()
    gradients(0, dw0, n, q)

    def rest(i, c):
        sum_gu.step(2 * n + i, n, 2 * n)
        d_step(dw0, (n + 1) // 2 + i, q)
        return c

    lax.fori_loop(0, HOPS, rest, 0)


def backward(dy, gu, d, pq, act, at, h, dw1):
    tokens, width = dy.shape
    n, hidden = gu.shape[0] // 2, dw1.shape[0]
    q = -(-(hidden // 32) // 16)
    assert q == (n + 1) // 2 and tokens // TILE >= HOPS
    any_space, vmem = pl.BlockSpec(memory_space=pl.ANY), pl.BlockSpec(memory_space=pltpu.VMEM)
    out = pl.pallas_call(
        backward_kernel,
        out_shape=[
            jax.ShapeDtypeStruct((2 * n, 64, TILE), BF16),
            jax.ShapeDtypeStruct((2 * q, 16, width), BF16),
            jax.ShapeDtypeStruct((n, 2, tokens, TILE), BF16),
            jax.ShapeDtypeStruct((hidden, width), BF16),
        ],
        in_specs=[any_space] * 8,
        out_specs=[vmem, vmem, any_space, any_space],
        scratch_shapes=[
            pltpu.VMEM((tokens, width), BF16),
            pltpu.VMEM((width, tokens), BF16),
            pltpu.VMEM((2, TILE, width), BF16),
        ]
        + [pltpu.SemaphoreType.DMA(()) for _ in range(4)]
        + [pltpu.SemaphoreType.DMA((2,)) for _ in range(7)]
        + Sum.scratch(64, TILE)
        + Sum.scratch(16, width),
        compiler_params=pltpu.CompilerParams(collective_id=1, has_side_effects=True, vmem_limit_bytes=VMEM_LIMIT),
        name="backward",
    )(dy, gu, d, pq, act, at, h, dw1)
    g_gu, g_d = out[:2]
    both = g_gu.reshape(2, n, 2, 32, TILE).transpose(0, 2, 3, 1, 4).reshape(2, 2, 32, hidden)
    down = g_d.reshape(2, q * 16, width)
    rows, kept = hidden // 32, 16 * (q - 1)
    down = jnp.concatenate([down[:, : rows - 16], down[:, kept:]], 1)
    return [one[::-1] for one in (both[:, 0], both[:, 1], down)]


def solution(mesh):
    def step(x, dy, *arrays):
        weights, m, v = (arrays[i : i + 3] for i in (0, 3, 6))
        gradients = [g.astype(F32) for g in backward(dy[0], *forward(x[0], dy[0], weights))]
        new = [adamw(w.astype(jnp.float32), m, v, g) for w, m, v, g in zip(weights, m, v, gradients, strict=True)]
        return tuple(one[which] for which in range(3) for one in new)

    states, cut = P(("rep", "r", "s"), None, None), P(None, "s", None)
    return jax.shard_map(
        step,
        mesh=mesh,
        in_specs=(states, states) + (cut,) * 9,
        out_specs=(P("rep", "s", None),) * 9,
        check_vma=False,
    )
```

time: 1040 us -> 422 us (0.41)
  waiting for transfers between devices: 605 us -> 0 us
  Pallas kernels: 0 us -> 408 us
  matrix products: 378 us -> 0 us
  local copies, waits for them, and re-layouts: 20.6 us -> 4.26 us
  between operations: 14.5 us -> 0.7 us
    pallas_call x0 -> x2, Pallas kernels: none -> 408 us  [the longest x1 249 us: backward(): pl.pallas_call(backward_kernel, out_shape=[jax.ShapeDtypeStruct((2 * n, 6...]
    reduce_scatter x6 -> x0, waiting for transfers between devices: 386 us -> none  [summed(): lax.psum_scatter(term, 's', scatter_dimension=0, tiled=True)]
    dot_general x15 -> x0, matrix products: 378 us -> none  [the longest x5 137 us: layer(): gate = jnp.dot(a, w['w_gate'], preferred_element_type=jnp.float32)]
    all_gather x6 -> x0, waiting for transfers between devices: 168 us -> none  [fetched(): lax.all_gather(w[number], 's', axis=0, tiled=True)]
    psum x1 -> x0, waiting for transfers between devices: 49.6 us -> none  [summed(): lax.psum(lax.psum_scatter(term, 's', scatter_dimension=0, tiled=True), 'r')]
    unnamed x30 -> x4, local copies, waits for them, and re-layouts: 15.1 us -> 0.01 us
  transfers between devices with their start and end apart: 13 -> 0, of which waited for: 12 -> 0; matrix products, arithmetic and copies ran while one was open for 28% -> 0% of each run, Pallas kernels for 0% -> 0%
where the time goes in v2:
time: 422 us; the launch traced here: 421 us
  Pallas kernels  408 us (97%)
  other arithmetic  7.52 us (2%)
  local copies, waits for them, and re-layouts  4.26 us (1%)
    pallas_call x1, Pallas kernels, backward(): pl.pallas_call(backward_kernel, out_shape=[jax.ShapeDtypeStruct((2 * n, 6...  249 us
    pallas_call x1, Pallas kernels, forward(): pl.pallas_call(forward_kernel, out_shape=[jax.ShapeDtypeStruct(*shape) fo...  160 us

profile of v2, /device:TPU:0, one launch (start us, length us, event | category | flops | bytes accessed | tf_op | source)
XLA Modules:
  0.0 420.9 jit_solution(10746381002858799099)
XLA Ops:
  0.6 159.6 %forward.1 = (bf16[26,4,4,2,64,256]{5,4,3,2,1,0:T(8,128)(2,1)}, bf16[8,3328,256]{2,1,0:T(8,128)(2,1)}, f32[26,2,2048,256]{3,2,1,0:T(8,128)}, bf16[13,2048,256]{2...) custom-call(bf16[2048,1024]{1,0:T(8,128)(2,1)} %bitcast.15, ...), custom_call_target="tpu_custom_call" | custom-call | tf_op jit(solution)/shard_map/forward/pallas_call | solution.py:404
  160.2 248.9 %backward.1 = (bf16[26,64,256]{2,1,0:T(8,128)(2,1)}, bf16[14,16,1024]{2,1,0:T(8,128)(2,1)}, bf16[13,2,2048,256]{3,2,1,0:T(8,128)(2,1)}, bf16[3328,1024]{1,0:T(8,128)(2,1)}) custom-call(bf16[2048,1024]{1,0:T(8,128)(2,1)} %bitcast.14, bf16[26,4,4,2,64,256]{5,4,3,2,1,0:T(8,128)(2,1)} %get-tuple-element.18.gu, bf16[8,3328,256]{2,1,0:T(8,128)(2,1)} %get-tuple-element.19.d, ...), custom_call_target="tpu_custom_call" | custom-call | tf_op jit(solution)/shard_map/backward/pallas_call | solution.py:730
  409.1 0.0 copy-start
  409.1 0.0 copy-start.1
  409.1 0.9 slice.19
  410.1 1.0 slice.18
  411.1 1.7 copy.25
  412.8 0.6 reshape.28
  413.4 0.1 slice_bitcast_fusion
  413.4 3.1 fusion.10
  416.6 0.0 copy-done
  416.6 0.0 copy-done.1
  416.6 4.4 %fusion.2 = (bf16[2,32,3328]{2,1,0:T(8,128)(2,1)}, f32[2,32,3328]{2,1,0:T(8,128)}, f32[2,32,3328]{2,1,0:T(8,128)}, bf16[2,32,3328]{2,1,0:T(8,128)(2,1)}, f32[2,32,3328]{2,1,0:T(8,128)}, /*index=5*/f32[2,32,3328]{2,1,0:T(8,128)}) fusion(bf16[2,32,3328]{2,1,0:T(8,128)(2,1)S(1)} %copy-done, bf16[2,32,3328]{2,1,0:T(8,128)(2,1)S(1)} %get-tuple-element.37, ...), kind=kLoop, calls=%fused_computation.15 | loop fusion | flops 6815744 | bytes 9371648 | tf_op jit(solution)/shard_map/convert_element_type | solution.py:24
  (1 shorter events, 0.0 us)
Async XLA Ops:
  409.1 7.5 %copy-start = (bf16[2,32,3328]{2,1,0:T(8,128)(2,1)S(1)}, bf16[2,32,3328]{2,1,0:T(8,128)(2,1)}, u32[]{:S(2)}) copy-start(bf16[2,32,3328]{2,1,0:T(8,128)(2,1)} %w_gate.1) | copy-start | bytes 1277956
  409.1 7.4 %copy-start.1 = (bf16[2,32,3328]{2,1,0:T(8,128)(2,1)S(1)}, bf16[2,32,3328]{2,1,0:T(8,128)(2,1)}, u32[]{:S(2)}) copy-start(bf16[2,32,3328]{2,1,0:T(8,128)(2,1)} %w_up.1) | copy-start | bytes 1277956

commit v3 on v2

v3 whole, which is shorter than its diff:
```python
import functools

import jax
import jax.numpy as jnp
from jax import lax
from jax.experimental import pallas as pl
from jax.experimental.pallas import tpu as pltpu
from jax.sharding import PartitionSpec as P

NAMES = ("w_gate", "w_up", "w_down")
MESH = pl.DeviceIdType.MESH
F32, BF16 = jnp.float32, jnp.bfloat16
HOPS = 6
VMEM_LIMIT = 67043328
PLAIN, BY_COLUMNS, BY_ROWS = (((1,), (0,)), ((), ())), (((1,), (1,)), ((), ())), (((0,), (0,)), ((), ()))
HERE, NEXT, FAR, LAST = range(4)
DOWN = 2
TILE = 256


def adamw(w, m, v, g):
    m = 0.9 * m + 0.1 * g
    v = 0.95 * v + 0.05 * g * g
    step = m * lax.rsqrt(v + 1e-8) + 0.1 * w
    return (w - 0.02 * step).astype(jnp.bfloat16), m, v


def dot(a, b, dims=PLAIN):
    return lax.dot_general(a, b, dims, preferred_element_type=F32)


def scoped(name):
    def wrap(f):
        @functools.wraps(f)
        def inner(*args, **kwargs):
            with jax.named_scope(name):
                return f(*args, **kwargs)

        return inner

    return wrap


def block(n, size=TILE):
    return pl.ds(pl.multiple_of(n * size, size), size)


def added(values):
    total = None
    for value in values:
        total = value if total is None else total + value
    return total


OTHERS = (NEXT, FAR, LAST)


class Place:
    def __init__(self):
        self.s, self.x = lax.axis_index("s"), lax.axis_index("r")
        self.core = lax.rem(self.s, 2)
        y, z = self.yz = lax.div(self.s, 8), lax.rem(lax.div(self.s, 2), 4)
        a = y * (1 - self.core) + z * self.core
        b = z * (1 - self.core) + y * self.core
        step_a, step_b = 4 - 3 * self.core, 1 + 3 * self.core
        self.a, self.b = [[lax.rem(at + d, 4) for d in range(4)] for at in (a, b)]
        self.chips = [[self.a[d] * step_a + self.b[e] * step_b for e in range(4)] for d in range(4)]
        self.devices = {(d, e): 2 * self.chips[d][e] + self.core for d in range(4) for e in range(4)}
        self.across = self.s + 1 - 2 * self.core

    def at(self, d, e):
        return {"s": self.devices[d, e]}

    def partner(self):
        return {"s": self.across}

    def pair(self, second):
        return {"r": 3 - self.x if second else self.x + 1 - 2 * lax.rem(self.x, 2)}

    def neighbours(self, far):
        around = [self.at(*there) for there in ((NEXT, HERE), (LAST, HERE), (HERE, NEXT), (HERE, LAST), *far)]
        return [self.partner()] + around


def meet(places):
    barrier = pltpu.get_barrier_semaphore()
    for place in places:
        pl.semaphore_signal(barrier, inc=1, device_id=place, device_id_type=MESH)
    pl.semaphore_wait(barrier, len(places))


def send(src, dst, send_sem, recv_sem, place):
    return pltpu.make_async_remote_copy(src_ref=src, dst_ref=dst, send_sem=send_sem, recv_sem=recv_sem, device_id=place, device_id_type=MESH)


class Gather:
    SLOTS = 12

    def __init__(self, p, n, m, here, full, sems):
        self.p, self.n, self.m, self.here, self.full = p, n, m, here, full
        self.out_sem, self.in_sem, self.here_sem, self.own_sem = sems
        self.total = 2 * (n + m)

    def hop(self, core, kind, hop, u, later):
        p, k = self.p, lax.rem(u, self.SLOTS)
        at = u - self.n * (1 + later) if kind == DOWN else u - (self.n + self.m) * later
        f = self.full[kind].at[at]
        here = self.here[kind].at[at] if kind else f.at[(*p.yz, core)]
        rows = here.shape[0]
        cut = (rows // 2 + 7) // 8 * 8
        low, high = (0, cut), (cut, rows - cut)

        def piece(d, e, half=(0, rows)):
            if kind == DOWN:
                return f.at[pl.ds(pl.multiple_of(rows * p.devices[d, e], 8) + half[0], half[1])]
            whole = f.at[p.a[d], p.b[e], core] if core == 0 else f.at[p.b[e], p.a[d], core]
            return whole.at[pl.ds(*half)]

        def group(e, half=(0, rows)):
            if kind == DOWN:
                return [piece(d, e, half) for d in range(4)]
            whole = f.at[:, p.b[e], core] if core == 0 else f.at[p.b[e], :, core]
            return [whole.at[:, pl.ds(*half)]]

        def of_size(lines, columns, half=(0, rows)):
            if kind == DOWN:
                return f.at[pl.ds(0, lines * columns * half[1])]
            return f.at[pl.ds(0, lines), pl.ds(0, columns), 0, pl.ds(*half)]

        def go(i, ref, place, left=0, src=None):
            send(ref if src is None else src, ref, self.out_sem.at[k, left], self.in_sem.at[k, i], place).start()

        def over(e):
            for one in group(e):
                go(8, one, p.partner(), FAR)

        def came(sem, ref):
            pltpu.make_async_copy(ref, ref, sem).wait()

        def all_came(i, columns, half=(0, rows)):
            came(self.in_sem.at[k, i], of_size(1, columns, half))

        sides = ((NEXT, LAST, low), (LAST, NEXT, high))
        if hop == 0:
            came(self.here_sem.at[u], here)
            own = piece(HERE, HERE)
            for side, (ahead, _, _) in enumerate(sides):
                go(side, own, p.at(ahead, HERE), src=here)
            if kind:
                pltpu.make_async_copy(here, own, self.own_sem.at[k]).start()
        if hop == 1:
            for side, (ahead, back, half) in enumerate(sides):
                all_came(side, 1)
                go(2 + side, piece(back, HERE, half), p.at(ahead, HERE))
        if hop == 2:
            if kind:
                came(self.own_sem.at[k], piece(HERE, HERE))
            for side, (_, _, half) in enumerate(sides):
                all_came(2 + side, 1, half)
            for one in group(HERE):
                for side, (ahead, _, _) in enumerate(sides):
                    go(4 + side, one, p.at(HERE, ahead), 1)
            over(HERE)
        if hop == 3:
            for side, (ahead, back, half) in enumerate(sides):
                all_came(4 + side, 4)
                for one in group(back, half):
                    go(6 + side, one, p.at(HERE, ahead), 1)
                over(back)
        if hop == 4:
            for side, (_, _, half) in enumerate(sides):
                all_came(6 + side, 4, half)
            over(FAR)
        if hop == 5:
            came(self.in_sem.at[k, 8], of_size(4, 4))
            for i, (lines, columns) in enumerate(((1, 3), (3, 4), (4, 4))):
                came(self.out_sem.at[k, i], of_size(lines, columns))

    EARLY, LATER = 2, 4

    def done(self, u):
        return u + 10 + (self.LATER if u >= self.EARLY else 0)

    @scoped("gather")
    def step(self, t):
        def both(core, hop, u):
            later = lax.div(u, self.n + self.m)
            is_down = u - (self.n + self.m) * later >= self.n
            for layer in range(2):
                pl.when(~is_down & (later == layer))(lambda layer=layer: self.hop(core, layer, hop, u, later))
            pl.when(is_down)(lambda: self.hop(core, DOWN, hop, u, later))

        def run(core):
            for hop in range(5, -1, -1):
                at = t - 2 * hop
                early = at < self.EARLY
                u = jnp.where(early, at, at - self.LATER)
                there = (at >= 0) & (u < self.total) & (early | (u >= self.EARLY))
                pl.when(there)(functools.partial(both, core, hop, u))

        for core in (0, 1):
            pl.when(self.p.core == core)(functools.partial(run, core))

    def steps(self, first, count):
        lax.fori_loop(0, count, lambda i, c: (self.step(first + i), c)[1], 0)


def normed(wide):
    return (wide * lax.rsqrt(jnp.mean(wide * wide, -1, keepdims=True) + 1e-6)).astype(BF16)


def forward_kernel(x, dy, w_gate, w_up, w_down, gu, d, pq, act_out, at_out, h_out, dw_out,
                   a, dyv, act, near, wt, wdt, pqs, h, ats, xs, dws, here, here_d, out_sem, in_sem, here_sem, own_sem,
                   x_sem, dy_sem, act_sem, h_sem, w_sem, wd_sem, pq_sem, at_sem, xs_sem, dw_sem):
    tokens, width = a.shape
    n, m = act.shape[0], h.shape[0]
    p = Place()
    gather = Gather(p, n, m, (None, here, here_d), (near, gu, d), (out_sem, in_sem, here_sem, own_sem))
    copy = pltpu.make_async_copy
    copy(x, a, x_sem).start()
    for layer in range(2):

        def bring(j, c, layer=layer):
            u = j + layer * (n + m)
            own = here.at[j] if layer else near.at[(j, *p.yz, p.core)]
            copy(w_gate.at[layer, :, block(j)], own.at[pl.ds(0, 32)], here_sem.at[u]).start()
            copy(w_up.at[layer, :, block(j)], own.at[pl.ds(32, 32)], here_sem.at[u]).start()
            return c

        lax.fori_loop(0, n, bring, 0)
        for i in range(m):
            u = n + i + layer * (n + m)
            copy(w_down.at[layer, :, pl.ds(i * TILE, TILE)], here_d.at[layer * m + i], here_sem.at[u]).start()
    copy(dy, dyv, dy_sem).start()
    meet(p.neighbours(()))

    def transposed(layer, i):
        return copy(ats.at[lax.rem(i, 2)], at_out.at[layer, :, block(i)], at_sem.at[lax.rem(i, 2)])

    @scoped("norm")
    def norm(layer, i, wide):
        value = normed(wide)
        a[block(i)] = value
        pl.when(i >= 2)(lambda: transposed(layer, i - 2).wait())
        ats[lax.rem(i, 2)] = value.T
        transposed(layer, i).start()

    def norm_done(layer):
        for i in (tokens // TILE - 2, tokens // TILE - 1):
            transposed(layer, i).wait()

    def start(t, c):
        gather.step(t)
        pl.when(t == 1)(lambda: copy(x, a, x_sem).wait())

        @pl.when((t >= 1) & (t <= tokens // TILE))
        def _():
            norm(0, t - 1, a[block(t - 1)].astype(F32))

        return c

    assert gather.done(0) >= tokens // TILE and gather.LATER == 4
    lax.fori_loop(0, gather.done(0) + 1, start, 0)
    norm_done(0)

    def w_tile(j, k):
        return copy(gu.at[j], wt.at[k], w_sem.at[k])

    def wd_tile(i, k):
        return copy(d.at[i], wdt.at[k], wd_sem.at[k])

    def x_tile(i, k):
        return copy(x.at[:, block(i)], xs.at[k], xs_sem.at[k])

    def pq_tile(layer, j, k):
        return copy(pqs.at[k], pq.at[layer * n + j], pq_sem.at[k])

    def dw_tile(j, k):
        return copy(dws.at[k], dw_out.at[block(j)], dw_sem.at[k])

    def act_tile(j):
        return copy(act.at[j], act_out.at[j], act_sem)

    base = gather.done(n + 1) + 2 * m

    def hidden(layer):
        def body(j, c):
            k = lax.rem(j, 2)
            if layer:
                gather.step(base + j)
            else:
                first = jnp.where(j < 3, gather.done(0) + 1 + 3 * (j - 1), gather.done(2) + j - 2)

                def more(i, c):
                    pl.when((j > 0) & ((i == 0) | (j < 3)))(lambda: gather.step(first + i))
                    return c

                lax.fori_loop(0, 3, more, 0)
            if layer:
                pl.when(j < n - 1)(lambda: w_tile(j + 1, 1 - k).start())
                w_tile(j, k).wait()
            else:

                @pl.when(j == n - 1)
                def _():
                    gather.step(gather.done(n))
                    wd_tile(0, 0).start()
                    x_tile(0, 0).start()

            pl.when(j >= 2 - 2 * layer)(lambda: pq_tile(layer, j, k).wait())
            if layer:
                pl.when(j >= 2)(lambda: dw_tile(j - 2, k).wait())
            with jax.named_scope("hidden"):
                w = wt.at[k] if layer else near.at[j]
                gate_w, up_w = (w[:, :, :, 32 * i : 32 * i + 32, :].reshape(width, TILE) for i in range(2))
                for i in range(tokens // 512):
                    rows = pl.ds(512 * i, 512)
                    gate, up = dot(a[rows], gate_w), dot(a[rows], up_w)
                    s = 0.5 * jnp.tanh(0.5 * gate) + 0.5
                    silu = gate * s
                    pqs[k, 0, rows] = silu
                    pqs[k, 1, rows] = up * (s + silu * (1 - s))
                    act[j, rows] = (silu * up).astype(BF16)
            if layer:

                @pl.when(j < n)
                @scoped("down_terms")
                def _():
                    dws[k] = dot(act[j], dyv[...], BY_ROWS).astype(BF16)

                dw_tile(j, k).start()
            else:
                act_tile(j).start()
            pq_tile(layer, j, k).start()
            return c

        lax.fori_loop(0, n, body, 0)
        if layer:
            for j in (n - 2, n - 1):
                pq_tile(layer, j, j % 2).wait()
                dw_tile(j, j % 2).wait()

    hidden(0)

    def h_tile(i):
        return copy(h.at[i], h_out.at[:, block(i)], h_sem)

    def down(i, c):
        k = lax.rem(i, 2)
        for more in range(2):
            gather.step(gather.done(n + 1) + 2 * i + more)

        @pl.when(i < m - 1)
        def _():
            wd_tile(i + 1, 1 - k).start()
            x_tile(i + 1, 1 - k).start()

        @pl.when(i == m - 1)
        def _():
            w_tile(0, 0).start()

        with jax.named_scope("tiles"):
            wd_tile(i, k).wait()
            x_tile(i, k).wait()
        with jax.named_scope("down"):
            for r in range(tokens // 512):
                rows = pl.ds(512 * r, 512)
                out = added(dot(act[j, rows], wdt[k, pl.ds(TILE * j, TILE)]) for j in range(n))
                h[i, rows] = xs[k, rows] + out.astype(BF16)
        h_tile(i).start()
        return c

    lax.fori_loop(0, m, down, 0)

    def norm_later(i, c):
        norm(1, i, jnp.concatenate([h[q, block(i)] for q in range(m)], -1).astype(F32))
        return c

    lax.fori_loop(0, tokens // TILE, norm_later, 0)
    norm_done(1)
    with jax.named_scope("between"):
        copy(act, act_out, act_sem).wait()
        copy(dy, dyv, dy_sem).wait()
    hidden(1)
    gather.steps(base + n, max(0, gather.done(gather.total - 1) + 1 - base - n))
    copy(h, h, h_sem).wait()


def forward(x, dy, weights):
    tokens, width = x.shape
    w_gate, w_up, w_down = weights
    hidden, rows = w_gate.shape[-1], w_down.shape[1]
    n, m = hidden // TILE, width // TILE
    layers, pieces = 2, (4, 4, 2, 64, TILE)
    shapes = [
        ((n, *pieces), BF16),
        ((layers * m, hidden, TILE), BF16),
        ((layers * n, 2, tokens, TILE), F32),
        ((n, tokens, TILE), BF16),
        ((layers, width, tokens), BF16),
        ((tokens, width), BF16),
        ((hidden, width), BF16),
    ]

    def twice(*shape, dtype=BF16):
        return pltpu.VMEM((2, *shape), dtype)

    def sems(*shape):
        return pltpu.SemaphoreType.DMA(shape)

    scratch = [
        pltpu.VMEM((tokens, width), BF16),
        pltpu.VMEM((tokens, width), BF16),
        pltpu.VMEM((n, tokens, TILE), BF16),
        pltpu.VMEM((n, *pieces), BF16),
        twice(*pieces),
        twice(hidden, TILE),
        twice(2, tokens, TILE, dtype=F32),
        pltpu.VMEM((m, tokens, TILE), BF16),
        twice(width, TILE),
        twice(tokens, TILE),
        twice(TILE, width),
        pltpu.VMEM((n, *pieces[3:]), BF16),
        pltpu.VMEM((layers * m, rows, TILE), BF16),
        sems(Gather.SLOTS, 3),
        sems(Gather.SLOTS, 9),
        sems(layers * (n + m)),
        sems(Gather.SLOTS),
    ]
    scratch += [sems() for _ in range(4)] + [sems(2) for _ in range(6)]
    return pl.pallas_call(
        forward_kernel,
        out_shape=[jax.ShapeDtypeStruct(*shape) for shape in shapes],
        in_specs=[pl.BlockSpec(memory_space=pl.ANY)] * 5,
        out_specs=[pl.BlockSpec(memory_space=pl.ANY)] * len(shapes),
        scratch_shapes=scratch,
        compiler_params=pltpu.CompilerParams(collective_id=0, has_side_effects=True, vmem_limit_bytes=VMEM_LIMIT),
        name="forward",
    )(x, dy, w_gate, w_up, w_down)


class Sum:
    @staticmethod
    def scratch(terms, slots, rows, columns):
        def many(slots, *lead, columns=columns, dtype=BF16, count=1):
            return [pltpu.VMEM((slots, *lead, rows, columns), dtype)] * count

        half, near = columns // 2, 2
        return (
            many(terms, 16, 2)
            + many(slots, 16)
            + many(slots, 4, dtype=F32)
            + many(near, 4, dtype=F32, count=2)
            + many(near, 4, count=3)
            + many(slots, 4, columns=half, count=2)
            + many(slots, 4, count=2)
            + many(slots, dtype=F32)
            + many(near, 3)
            + many(slots, 3)
            + many(near, count=2)
            + many(slots, count=2)
            + [pltpu.SemaphoreType.DMA((slots, 10))] * 2
        )

    def __init__(self, p, refs, emit, lag, delay):
        self.p, self.emit, self.lag, self.delay = p, emit, lag, delay
        self.term, self.swapped, self.ca, self.cp, self.cm, self.x1, self.x2p, self.x2m, self.r1a, self.r1b, self.r2p, self.r2m = refs[:12]
        self.db, self.y, self.ry, self.z, self.w, self.rz, self.rw = refs[12:19]
        self.out_sem, self.in_sem = refs[19:]
        self.half = self.term.shape[-1] // 2

    def slot(self, ref, u):
        return ref.at[lax.rem(u, ref.shape[0])]

    def copies(self, hop, u):
        p, h = self.p, self.half
        out_sem, in_sem = self.slot(self.out_sem, u), self.slot(self.in_sem, u)

        def one(i, src, dst, place):
            return send(src, dst, out_sem.at[i], in_sem.at[i], place)

        if hop == 0:
            return [one(0, self.slot(self.term, u).at[:, 1 - p.core], self.slot(self.swapped, u), p.partner())]
        if hop == 3:
            y, ry = self.slot(self.y, u), self.slot(self.ry, u)
            return [one(5 + i, y.at[i], ry.at[i], p.at(HERE, ahead)) for i, ahead in enumerate(OTHERS)]
        if hop > 3:
            second = hop == 5
            src, dst = (self.w, self.rw) if second else (self.z, self.rz)
            return [one(4 + hop, self.slot(src, u), self.slot(dst, u), p.pair(second))]
        sources, landings = ((self.x1, self.x1), (self.r1a, self.r1b)) if hop == 1 else ((self.x2p, self.x2m), (self.r2p, self.r2m))
        made = []
        for side, (src, dst, ahead) in enumerate(zip(sources, landings, (NEXT, LAST), strict=True)):
            src = self.slot(src, u)
            if hop == 1:
                src = src.at[:, :, pl.ds(side * h, h)]
            made.append(one(2 * hop - 1 + side, src, self.slot(dst, u), p.at(ahead, HERE)))
        return made

    def add(self, hop, u):
        p, h = self.p, self.half
        low, high = slice(0, h), slice(h, None)

        def of(ref, *index):
            return ref[(lax.rem(u, ref.shape[0]), *index)].astype(F32)

        def put(ref, value, *index):
            ref[(lax.rem(u, ref.shape[0]), *index)] = value.astype(ref.dtype)

        rows = slice(None)
        if hop == 1:
            for d, ref in enumerate((self.ca, self.cp, self.x1, self.cm)):
                for e in range(4):
                    chip = p.chips[d][e]
                    put(ref, of(self.term, chip, p.core) + of(self.swapped, chip), e)
        if hop == 2:
            for e in range(4):
                put(self.x2p, of(self.cp, e, rows, low) + of(self.r1a, e), e, rows, low)
                put(self.x2p, of(self.cp, e, rows, high), e, rows, high)
                put(self.x2m, of(self.cm, e, rows, low), e, rows, low)
                put(self.x2m, of(self.cm, e, rows, high) + of(self.r1b, e), e, rows, high)
        if hop == 3:
            for e in range(4):
                value = of(self.ca, e) + of(self.r2p, e) + of(self.r2m, e)
                put(self.y, value, e - 1) if e else put(self.db, value)
        if hop == 4:
            put(self.z, (of(self.db) + of(self.ry, 0)) + (of(self.ry, 1) + of(self.ry, 2)))
        if hop == 5:
            put(self.w, of(self.z) + of(self.rz))
        if hop == 6:
            self.emit(u, (of(self.w) + of(self.rw)).astype(BF16))

    def hop(self, hop, u):
        with jax.named_scope(f"hop{hop}"):
            self.do(hop, u)

    def do(self, hop, u):
        if hop:
            for copy in self.copies(hop - 1, u):
                copy.wait()
        self.add(hop, u)
        if hop < HOPS:
            for copy in self.copies(hop, u):
                copy.start()

    def step(self, t, first, last):
        for hop in range(HOPS, -self.delay, -1):
            u = t - self.delay - self.lag * hop
            pl.when((u >= first) & (u < last))(functools.partial(self.hop, hop, u))


def backward_kernel(dy, gu, d, pq, act, at, h, dw1, g_gate, g_up, g_down, dgu_out, dw0, dh, av, big, load_sem, dh_sem, at_sem, big_sem, wd_sem, pq_sem, dgu_sem, dw_sem, dgc_sem, h_sem, *scratch):
    tokens, width = dh.shape
    n, m, d_rows = act.shape[0], width // TILE, g_down.shape[1]
    half = len(scratch) // 2
    copy = pltpu.make_async_copy
    p = Place()

    def emit_gu(u, value):
        later = lax.div(u, n)
        for i, out in enumerate((g_gate, g_up)):
            out[1 - later, :, block(u - n * later)] = value[32 * i : 32 * i + 32]

    def emit_d(u, value):
        later = lax.div(u, m)
        g_down[1 - later, :, block(u - m * later)] = value

    sum_gu, sum_d = Sum(p, scratch[:half], emit_gu, 2, 1), Sum(p, scratch[half:], emit_d, 1, 0)
    copy(dy, dh, dh_sem).start()
    copy(at.at[1], av, at_sem).start()

    def d_start(term, s, first):
        def one(i, c):
            rows = pl.ds(pl.multiple_of(d_rows * i, 8), d_rows)
            copy(term.at[rows, block(s)], sum_d.term.at[lax.rem(first + s, 2), lax.div(i, 2), lax.rem(i, 2)], load_sem).start()
            return c

        lax.fori_loop(0, 32, one, 0)

    def d_step(term, s, first, ready=None):
        sum_d.step(first + s, first, first + m)

        @pl.when(s < m)
        def _():
            whole = sum_d.term.at[lax.rem(first + s, 2)]
            copy(whole, whole, load_sem).wait()
            sum_d.hop(0, first + s)

        @pl.when(s + 1 < m)
        def _():
            if ready is not None:
                ready(s + 1)
            d_start(term, s + 1, first)

    def gradients(layer, first, begin, d_turn):
        def phase(wdt, pqt, dgu):
            def tiles(j, k):
                return [
                    copy(d.at[pl.ds(layer * m, m), block(j)], wdt.at[k], wd_sem.at[k]),
                    copy(pq.at[layer * n + j], pqt.at[k], pq_sem.at[k]),
                ]

            def dgu_tile(j, k):
                return copy(dgu.at[k], dgu_out.at[j], dgu_sem.at[k])

            def body(j, c):
                k = lax.rem(j, 2)
                sum_gu.step(first + j, first, first + n)
                d_turn(j)
                if layer:
                    copy(gu.at[j], big.at[j], big_sem.at[0]).start()

                @pl.when(j < n - 1)
                def _():
                    for one in tiles(j + 1, 1 - k):
                        one.start()

                with jax.named_scope("tiles"):
                    for one in tiles(j, k):
                        one.wait()
                    if layer:
                        pl.when(j >= 2)(lambda: dgu_tile(j - 2, k).wait())
                with jax.named_scope("terms"):
                    for i in range(tokens // 512):
                        rows = pl.ds(512 * i, 512)
                        by_act = added(dot(dh[rows, TILE * e : TILE * e + TILE], wdt[k, e], BY_COLUMNS) for e in range(m))
                        by_act = by_act.astype(BF16).astype(F32)
                        dgu[k, 0, rows] = (by_act * pqt[k, 1, rows]).astype(BF16)
                        dgu[k, 1, rows] = (by_act * pqt[k, 0, rows]).astype(BF16)
                    slot = lax.rem(first + j, sum_gu.term.shape[0])
                    for i in range(m):
                        for e in (0, 1):
                            value = dot(av[TILE * i : TILE * i + TILE], dgu[k, e]).astype(BF16)
                            sum_gu.term[slot, 4 * i : 4 * i + 4, :, 32 * e : 32 * e + 32, :] = value.reshape(4, 2, 32, TILE)
                if layer:
                    dgu_tile(j, k).start()
                return c

            for one in tiles(0, 0):
                one.start()
            begin()
            lax.fori_loop(0, n, body, 0)
            if layer:
                for j in (n - 2, n - 1):
                    dgu_tile(j, j % 2).wait()

        pl.run_scoped(
            phase,
            pltpu.VMEM((2, m, TILE, TILE), BF16),
            pltpu.VMEM((2, 2, tokens, TILE), F32),
            pltpu.VMEM((2, 2, tokens, TILE), BF16),
        )

    def to_states(dgc, hv):
        def rows_in(i, k):
            return [
                copy(dgu_out.at[:, :, block(i)], dgc.at[k], dgc_sem.at[k]),
                copy(h.at[block(i)], hv.at[k], h_sem.at[k]),
            ]

        def body(i, c):
            k = lax.rem(i, 2)
            sum_gu.step(n + i, 0, n)
            pl.when(k == 0)(lambda: d_step(dw1, (n + 1) // 2 + lax.div(i, 2), 0))

            @pl.when(i < tokens // TILE - 1)
            def _():
                for one in rows_in(i + 1, 1 - k):
                    one.start()

            with jax.named_scope("tiles"):
                for one in rows_in(i, k):
                    one.wait()
            with jax.named_scope("states"):
                parts = []
                for e in range(m):
                    weights = [big[j, 2 * TILE * e : 2 * TILE * (e + 1)].reshape(8, 64, TILE) for j in range(n)]
                    two = [
                        added(dot(dgc[k, j, o], weights[j][:, 32 * o : 32 * o + 32].reshape(TILE, TILE), BY_COLUMNS) for j in range(n))
                        for o in (0, 1)
                    ]
                    parts.append((two[0].astype(BF16) + two[1].astype(BF16)).astype(F32))
                by_a = jnp.concatenate(parts, -1)
                wide = hv[k].astype(F32)
                scale = lax.rsqrt(jnp.mean(wide * wide, -1, keepdims=True) + 1e-6)
                along = jnp.mean(by_a * wide, -1, keepdims=True)
                by_h = by_a * scale - wide * (scale * scale * scale * along)
                dh[block(i)] = dh[block(i)] + by_h.astype(BF16)
            return c

        for one in rows_in(0, 0):
            one.start()
        with jax.named_scope("weights"):
            copy(gu, big, big_sem.at[0]).wait()
        lax.fori_loop(0, tokens // TILE, body, 0)

    def down(turned, made):
        def out(e):
            return copy(made.at[lax.rem(e, 2)], dw0.at[:, block(e)], dw_sem.at[lax.rem(e, 2)])

        def body(e, c):
            k = lax.rem(e, 2)
            for i in (0, 1):
                sum_gu.step(n + tokens // TILE + 2 * e + i, 0, n)

            @pl.when(e == 1)
            def _():
                out(0).wait()
                d_start(dw0, 0, m)

            pl.when(e >= 2)(lambda: d_step(dw0, e - 2, m, lambda s: out(s).wait()))
            with jax.named_scope("turn"):
                turned[...] = dh[:, block(e)].T

            pl.when(e == 0)(lambda: copy(act, big, big_sem.at[0]).wait())
            with jax.named_scope("down_terms"):
                for j in range(n):
                    made[k, TILE * j : TILE * (j + 1)] = dot(turned[...], big[j]).astype(BF16).T
            out(e).start()
            return c

        copy(act, big, big_sem.at[0]).start()
        lax.fori_loop(0, m, body, 0)

        def last_turn(j):
            pl.when(lax.rem(j, 2) == 0)(lambda: d_step(dw0, 2 + lax.div(j, 2), m, lambda s: out(s).wait()))

        copy(at.at[0], av, at_sem).wait()
        gradients(0, n, lambda: None, last_turn)

    @scoped("meet")
    def begin():
        meet(p.neighbours(((HERE, FAR),)) + [p.pair(False), p.pair(True)])
        copy(dy, dh, dh_sem).wait()
        copy(at.at[1], av, at_sem).wait()

    def turn(j):
        pl.when(lax.rem(j, 2) == 0)(lambda: d_step(dw1, lax.div(j, 2), 0))

    d_start(dw1, 0, 0)
    gradients(1, 0, begin, turn)
    copy(at.at[0], av, at_sem).start()
    pl.run_scoped(
        to_states,
        pltpu.VMEM((2, n, 2, TILE, TILE), BF16),
        pltpu.VMEM((2, TILE, width), BF16),
    )
    pl.run_scoped(down, pltpu.VMEM((TILE, tokens), BF16), pltpu.VMEM((2, 32 * d_rows, TILE), BF16))

    def rest(i, c):
        sum_gu.step(2 * n + i, n, 2 * n)
        pl.when(i == 1)(lambda: d_step(dw0, (n + 1) // 2 + 2, m, lambda s: None))
        return c

    lax.fori_loop(0, 2 * HOPS + 1, rest, 0)


def backward(dy, gu, d, pq, act, at, h, dw1):
    tokens, width = dy.shape
    n, hidden = gu.shape[0], dw1.shape[0]
    rows, m = hidden // 32, width // TILE
    gu = gu.reshape(n, tokens, TILE)
    assert 32 * 64 == tokens and n + 2 == 3 * m + 3 and 2 * HOPS + 1 <= tokens // TILE + 2 * m
    any_space, vmem = pl.BlockSpec(memory_space=pl.ANY), pl.BlockSpec(memory_space=pltpu.VMEM)
    shapes = [((2, 32, hidden), BF16)] * 2 + [((2, rows, width), BF16), ((n, 2, tokens, TILE), BF16), ((hidden, width), BF16)]
    out = pl.pallas_call(
        backward_kernel,
        out_shape=[jax.ShapeDtypeStruct(*shape) for shape in shapes],
        in_specs=[any_space] * 8,
        out_specs=[vmem] * 3 + [any_space] * 2,
        scratch_shapes=[pltpu.VMEM(shape, BF16) for shape in ((tokens, width), (width, tokens), (n, tokens, TILE))]
        + [pltpu.SemaphoreType.DMA(())] * 3
        + [pltpu.SemaphoreType.DMA((2,))] * 7
        + Sum.scratch(3, 4, 64, TILE)
        + Sum.scratch(2, 2, rows, TILE),
        compiler_params=pltpu.CompilerParams(collective_id=1, has_side_effects=True, vmem_limit_bytes=VMEM_LIMIT),
        name="backward",
    )(dy, gu, d, pq, act, at, h, dw1)
    return out[:3]


def solution(mesh):
    def step(x, dy, *arrays):
        weights, m, v = (arrays[i : i + 3] for i in (0, 3, 6))
        gradients = backward(dy[0], *forward(x[0], dy[0], weights))
        new = [adamw(w.astype(F32), m, v, g.astype(F32)) for w, m, v, g in zip(weights, m, v, gradients, strict=True)]
        return tuple(one[which] for which in range(3) for one in new)

    states, cut = P(("rep", "r", "s"), None, None), P(None, "s", None)
    return jax.shard_map(
        step,
        mesh=mesh,
        in_specs=(states, states) + (cut,) * 9,
        out_specs=(P("rep", "s", None),) * 9,
        check_vma=False,
    )
```

time: 422 us -> 393 us (0.931)
  Pallas kernels: 408 us -> 384 us
  local copies, waits for them, and re-layouts: 4.26 us -> 0 us
    pallas_call x1, Pallas kernels: 249 us -> 212 us  [backward(): pl.pallas_call(backward_kernel, out_shape=[jax.ShapeDtypeStruct(*shape) f...]
    pallas_call x1, Pallas kernels: 160 us -> 172 us  [forward(): pl.pallas_call(forward_kernel, out_shape=[jax.ShapeDtypeStruct(*shape) fo...]
where the time goes in v3:
time: 393 us
  Pallas kernels  384 us (98%)
  other arithmetic  8.12 us (2%)
    pallas_call x1, Pallas kernels, backward(): pl.pallas_call(backward_kernel, out_shape=[jax.ShapeDtypeStruct(*shape) f...  212 us
    pallas_call x1, Pallas kernels, forward(): pl.pallas_call(forward_kernel, out_shape=[jax.ShapeDtypeStruct(*shape) fo...  172 us
    convert_element_type x2, other arithmetic, adamw(): return ((w - 0.02 * step).astype(jnp.bfloat16), m, v)  8.12 us

profile of v3, /device:TPU:0, one launch (start us, length us, event | category | flops | bytes accessed | tf_op | source)
XLA Modules:
  0.0 393.2 jit_solution(7599832930728952118)
XLA Ops:
  0.6 172.4 %forward.1 = (bf16[13,4,4,2,64,256]{5,4,3,2,1,0:T(8,128)(2,1)}, bf16[8,3328,256]{2,1,0:T(8,128)(2,1)}, f32[26,2,2048,256]{3,2,1,0:T(8,128)}, bf16[13,2048,256]{2...) custom-call(bf16[2048,1024]{1,0:T(8,128)(2,1)} %bitcast.6, ...), custom_call_target="tpu_custom_call" | custom-call | tf_op jit(solution)/shard_map/forward/pallas_call | solution.py:431
  173.1 212.0 %backward.1 = (bf16[2,32,3328]{2,1,0:T(8,128)(2,1)}, bf16[2,32,3328]{2,1,0:T(8,128)(2,1)}, bf16[2,104,1024]{2,1,0:T(8,128)(2,1)}, bf16[13,2,2048,256]{3,2,1,0:T(8,128)(2,1)}, bf16[3328,1024]{1,0:T(8,128)(2,1)}) custom-call(bf16[2048,1024]{1,0:T(8,128)(2,1)} %bitcast.4, bf16[13,2048,256]{2,1,0:T(8,128)(2,1)} %bitcast.5, ...), custom_call_target="tpu_custom_call" | custom-call | tf_op jit(solution)/shard_map/backward/pallas_call | solution.py:766
  385.0 3.3 fusion.10
  388.3 4.9 %fusion.2 = (bf16[2,32,3328]{2,1,0:T(8,128)(2,1)}, f32[2,32,3328]{2,1,0:T(8,128)}, f32[2,32,3328]{2,1,0:T(8,128)}, bf16[2,32,3328]{2,1,0:T(8,128)(2,1)}, f32[2,32,3328]{2,1,0:T(8,128)}, /*index=5*/f32[2,32,3328]{2,1,0:T(8,128)}) fusion(bf16[2,32,3328]{2,1,0:T(8,128)(2,1)} %w_gate.1, bf16[2,32,3328]{2,1,0:T(8,128)(2,1)} %get-tuple-element.26, ...), kind=kLoop, calls=%fused_computation.14 | loop fusion | flops 6815744 | bytes 9371648 | tf_op jit(solution)/shard_map/convert_element_type | solution.py:25

commit v4 on v3

--- a/solution.py
+++ b/solution.py
@@ -176,10 +176,8 @@
             for i, (lines, columns) in enumerate(((1, 3), (3, 4), (4, 4))):
                 came(self.out_sem.at[k, i], of_size(lines, columns))
 
-    EARLY, LATER = 2, 4
-
     def done(self, u):
-        return u + 10 + (self.LATER if u >= self.EARLY else 0)
+        return u + 10
 
     @scoped("gather")
     def step(self, t):
@@ -192,11 +190,8 @@
 
         def run(core):
             for hop in range(5, -1, -1):
-                at = t - 2 * hop
-                early = at < self.EARLY
-                u = jnp.where(early, at, at - self.LATER)
-                there = (at >= 0) & (u < self.total) & (early | (u >= self.EARLY))
-                pl.when(there)(functools.partial(both, core, hop, u))
+                u = t - 2 * hop
+                pl.when((u >= 0) & (u < self.total))(functools.partial(both, core, hop, u))
 
         for core in (0, 1):
             pl.when(self.p.core == core)(functools.partial(run, core))
@@ -259,8 +254,8 @@
 
         return c
 
-    assert gather.done(0) >= tokens // TILE and gather.LATER == 4
-    lax.fori_loop(0, gather.done(0) + 1, start, 0)
+    assert gather.done(0) >= tokens // TILE
+    lax.fori_loop(0, gather.done(0), start, 0)
     norm_done(0)
 
     def w_tile(j, k):
@@ -286,16 +281,7 @@
     def hidden(layer):
         def body(j, c):
             k = lax.rem(j, 2)
-            if layer:
-                gather.step(base + j)
-            else:
-                first = jnp.where(j < 3, gather.done(0) + 1 + 3 * (j - 1), gather.done(2) + j - 2)
-
-                def more(i, c):
-                    pl.when((j > 0) & ((i == 0) | (j < 3)))(lambda: gather.step(first + i))
-                    return c
-
-                lax.fori_loop(0, 3, more, 0)
+            gather.step(base + j if layer else gather.done(0) + j)
             if layer:
                 pl.when(j < n - 1)(lambda: w_tile(j + 1, 1 - k).start())
                 w_tile(j, k).wait()
@@ -694,7 +680,7 @@
             copy(gu, big, big_sem.at[0]).wait()
         lax.fori_loop(0, tokens // TILE, body, 0)
 
-    def down(turned, made):
+    def down(turned, made, load_sems):
         def out(e):
             return copy(made.at[lax.rem(e, 2)], dw0.at[:, block(e)], dw_sem.at[lax.rem(e, 2)])
 
@@ -712,14 +698,27 @@
             with jax.named_scope("turn"):
                 turned[...] = dh[:, block(e)].T
 
-            pl.when(e == 0)(lambda: copy(act, big, big_sem.at[0]).wait())
             with jax.named_scope("down_terms"):
-                for j in range(n):
-                    made[k, TILE * j : TILE * (j + 1)] = dot(turned[...], big[j]).astype(BF16).T
+
+                @pl.when(e == 0)
+                def _():
+                    def one(j, c):
+                        copy(act.at[j], big.at[j], load_sems.at[j]).wait()
+                        made[k, block(j)] = dot(turned[...], big[j]).astype(BF16).T
+                        return c
+
+                    lax.fori_loop(0, n, one, 0)
+
+                @pl.when(e > 0)
+                def _():
+                    for j in range(n):
+                        made[k, TILE * j : TILE * (j + 1)] = dot(turned[...], big[j]).astype(BF16).T
+
             out(e).start()
             return c
 
-        copy(act, big, big_sem.at[0]).start()
+        for j in range(n):
+            copy(act.at[j], big.at[j], load_sems.at[j]).start()
         lax.fori_loop(0, m, body, 0)
 
         def last_turn(j):
@@ -745,7 +744,7 @@
         pltpu.VMEM((2, n, 2, TILE, TILE), BF16),
         pltpu.VMEM((2, TILE, width), BF16),
     )
-    pl.run_scoped(down, pltpu.VMEM((TILE, tokens), BF16), pltpu.VMEM((2, 32 * d_rows, TILE), BF16))
+    pl.run_scoped(down, pltpu.VMEM((TILE, tokens), BF16), pltpu.VMEM((2, 32 * d_rows, TILE), BF16), pltpu.SemaphoreType.DMA((n,)))
 
     def rest(i, c):
         sum_gu.step(2 * n + i, n, 2 * n)

time: 393 us -> 384 us (0.977)
  Pallas kernels: 384 us -> 376 us
    pallas_call x1, Pallas kernels: 172 us -> 164 us  [forward(): pl.pallas_call(forward_kernel, out_shape=[jax.ShapeDtypeStruct(*shape) fo...]
where the time goes in v4:
time: 384 us
  Pallas kernels  376 us (98%)
  other arithmetic  8.12 us (2%)
    pallas_call x1, Pallas kernels, backward(): pl.pallas_call(backward_kernel, out_shape=[jax.ShapeDtypeStruct(*shape) f...  212 us
    pallas_call x1, Pallas kernels, forward(): pl.pallas_call(forward_kernel, out_shape=[jax.ShapeDtypeStruct(*shape) fo...  164 us
    convert_element_type x2, other arithmetic, adamw(): return ((w - 0.02 * step).astype(jnp.bfloat16), m, v)  8.12 us

profile of v4, /device:TPU:0, one launch (start us, length us, event | category | flops | bytes accessed | tf_op | source)
XLA Modules:
  0.0 384.3 jit_solution(3334822137835004023)
XLA Ops:
  0.6 163.9 %forward.1 = (bf16[13,4,4,2,64,256]{5,4,3,2,1,0:T(8,128)(2,1)}, bf16[8,3328,256]{2,1,0:T(8,128)(2,1)}, f32[26,2,2048,256]{3,2,1,0:T(8,128)}, bf16[13,2048,256]{2...) custom-call(bf16[2048,1024]{1,0:T(8,128)(2,1)} %bitcast.6, ...), custom_call_target="tpu_custom_call" | custom-call | tf_op jit(solution)/shard_map/forward/pallas_call | solution.py:417
  164.6 211.6 %backward.1 = (bf16[2,32,3328]{2,1,0:T(8,128)(2,1)}, bf16[2,32,3328]{2,1,0:T(8,128)(2,1)}, bf16[2,104,1024]{2,1,0:T(8,128)(2,1)}, bf16[13,2,2048,256]{3,2,1,0:T(8,128)(2,1)}, bf16[3328,1024]{1,0:T(8,128)(2,1)}) custom-call(bf16[2048,1024]{1,0:T(8,128)(2,1)} %bitcast.4, bf16[13,2048,256]{2,1,0:T(8,128)(2,1)} %bitcast.5, ...), custom_call_target="tpu_custom_call" | custom-call | tf_op jit(solution)/shard_map/backward/pallas_call | solution.py:765
  376.2 3.3 fusion.10
  379.5 4.9 %fusion.2 = (bf16[2,32,3328]{2,1,0:T(8,128)(2,1)}, f32[2,32,3328]{2,1,0:T(8,128)}, f32[2,32,3328]{2,1,0:T(8,128)}, bf16[2,32,3328]{2,1,0:T(8,128)(2,1)}, f32[2,32,3328]{2,1,0:T(8,128)}, /*index=5*/f32[2,32,3328]{2,1,0:T(8,128)}) fusion(bf16[2,32,3328]{2,1,0:T(8,128)(2,1)} %w_gate.1, bf16[2,32,3328]{2,1,0:T(8,128)(2,1)} %get-tuple-element.26, ...), kind=kLoop, calls=%fused_computation.14 | loop fusion | flops 6815744 | bytes 9371648 | tf_op jit(solution)/shard_map/convert_element_type | solution.py:25

commit v5 on v3

--- a/solution.py
+++ b/solution.py
@@ -10,11 +10,10 @@
 NAMES = ("w_gate", "w_up", "w_down")
 MESH = pl.DeviceIdType.MESH
 F32, BF16 = jnp.float32, jnp.bfloat16
-HOPS = 6
+HOPS = 5
 VMEM_LIMIT = 67043328
 PLAIN, BY_COLUMNS, BY_ROWS = (((1,), (0,)), ((), ())), (((1,), (1,)), ((), ())), (((0,), (0,)), ((), ()))
 HERE, NEXT, FAR, LAST = range(4)
-DOWN = 2
 TILE = 256
 
 
@@ -59,7 +58,7 @@
     def __init__(self):
         self.s, self.x = lax.axis_index("s"), lax.axis_index("r")
         self.core = lax.rem(self.s, 2)
-        y, z = self.yz = lax.div(self.s, 8), lax.rem(lax.div(self.s, 2), 4)
+        y, z = lax.div(self.s, 8), lax.rem(lax.div(self.s, 2), 4)
         a = y * (1 - self.core) + z * self.core
         b = z * (1 - self.core) + y * self.core
         step_a, step_b = 4 - 3 * self.core, 1 + 3 * self.core
@@ -74,11 +73,11 @@
     def partner(self):
         return {"s": self.across}
 
-    def pair(self, second):
-        return {"r": 3 - self.x if second else self.x + 1 - 2 * lax.rem(self.x, 2)}
+    def along_x(self, d):
+        return {"r": lax.rem(self.x + d, 4)}
 
     def neighbours(self, far):
-        around = [self.at(*there) for there in ((NEXT, HERE), (LAST, HERE), (HERE, NEXT), (HERE, LAST), *far)]
+        around = [self.at(*there) for there in ((NEXT, HERE), (LAST, HERE), (HERE, NEXT), (HERE, LAST), far)]
         return [self.partner()] + around
 
 
@@ -94,7 +93,7 @@
 
 
 class Gather:
-    SLOTS = 12
+    SLOTS = 10
 
     def __init__(self, p, n, m, here, full, sems):
         self.p, self.n, self.m, self.here, self.full = p, n, m, here, full
@@ -103,27 +102,27 @@
 
     def hop(self, core, kind, hop, u, later):
         p, k = self.p, lax.rem(u, self.SLOTS)
-        at = u - self.n * (1 + later) if kind == DOWN else u - (self.n + self.m) * later
+        at = u - self.m * later if kind == 0 else u - self.n * (1 + later)
+        here = self.here[kind].at[at]
+        rows = here.shape[0]
         f = self.full[kind].at[at]
-        here = self.here[kind].at[at] if kind else f.at[(*p.yz, core)]
-        rows = here.shape[0]
         cut = (rows // 2 + 7) // 8 * 8
         low, high = (0, cut), (cut, rows - cut)
 
         def piece(d, e, half=(0, rows)):
-            if kind == DOWN:
+            if kind:
                 return f.at[pl.ds(pl.multiple_of(rows * p.devices[d, e], 8) + half[0], half[1])]
             whole = f.at[p.a[d], p.b[e], core] if core == 0 else f.at[p.b[e], p.a[d], core]
             return whole.at[pl.ds(*half)]
 
         def group(e, half=(0, rows)):
-            if kind == DOWN:
+            if kind:
                 return [piece(d, e, half) for d in range(4)]
             whole = f.at[:, p.b[e], core] if core == 0 else f.at[p.b[e], :, core]
             return [whole.at[:, pl.ds(*half)]]
 
         def of_size(lines, columns, half=(0, rows)):
-            if kind == DOWN:
+            if kind:
                 return f.at[pl.ds(0, lines * columns * half[1])]
             return f.at[pl.ds(0, lines), pl.ds(0, columns), 0, pl.ds(*half)]
 
@@ -132,7 +131,7 @@
 
         def over(e):
             for one in group(e):
-                go(8, one, p.partner(), FAR)
+                go(7, one, p.partner(), FAR)
 
         def came(sem, ref):
             pltpu.make_async_copy(ref, ref, sem).wait()
@@ -144,59 +143,47 @@
         if hop == 0:
             came(self.here_sem.at[u], here)
             own = piece(HERE, HERE)
-            for side, (ahead, _, _) in enumerate(sides):
-                go(side, own, p.at(ahead, HERE), src=here)
-            if kind:
-                pltpu.make_async_copy(here, own, self.own_sem.at[k]).start()
+            for i, ahead in enumerate(OTHERS):
+                go(i, own, p.at(ahead, HERE), src=here)
+            pltpu.make_async_copy(here, own, self.own_sem.at[k]).start()
         if hop == 1:
-            for side, (ahead, back, half) in enumerate(sides):
-                all_came(side, 1)
-                go(2 + side, piece(back, HERE, half), p.at(ahead, HERE))
-        if hop == 2:
-            if kind:
-                came(self.own_sem.at[k], piece(HERE, HERE))
-            for side, (_, _, half) in enumerate(sides):
-                all_came(2 + side, 1, half)
+            came(self.own_sem.at[k], piece(HERE, HERE))
+            for i, _ in enumerate(OTHERS):
+                all_came(i, 1)
             for one in group(HERE):
                 for side, (ahead, _, _) in enumerate(sides):
-                    go(4 + side, one, p.at(HERE, ahead), 1)
+                    go(3 + side, one, p.at(HERE, ahead), 1)
             over(HERE)
+        if hop == 2:
+            for side, (ahead, back, half) in enumerate(sides):
+                all_came(3 + side, 4)
+                for one in group(back, half):
+                    go(5 + side, one, p.at(HERE, ahead), 1)
+                over(back)
         if hop == 3:
-            for side, (ahead, back, half) in enumerate(sides):
-                all_came(4 + side, 4)
-                for one in group(back, half):
-                    go(6 + side, one, p.at(HERE, ahead), 1)
-                over(back)
+            for side, (_, _, half) in enumerate(sides):
+                all_came(5 + side, 4, half)
+            over(FAR)
         if hop == 4:
-            for side, (_, _, half) in enumerate(sides):
-                all_came(6 + side, 4, half)
-            over(FAR)
-        if hop == 5:
-            came(self.in_sem.at[k, 8], of_size(4, 4))
+            came(self.in_sem.at[k, 7], of_size(4, 4))
             for i, (lines, columns) in enumerate(((1, 3), (3, 4), (4, 4))):
                 came(self.out_sem.at[k, i], of_size(lines, columns))
 
-    EARLY, LATER = 2, 4
-
     def done(self, u):
-        return u + 10 + (self.LATER if u >= self.EARLY else 0)
+        return u + 8
 
     @scoped("gather")
     def step(self, t):
         def both(core, hop, u):
             later = lax.div(u, self.n + self.m)
             is_down = u - (self.n + self.m) * later >= self.n
-            for layer in range(2):
-                pl.when(~is_down & (later == layer))(lambda layer=layer: self.hop(core, layer, hop, u, later))
-            pl.when(is_down)(lambda: self.hop(core, DOWN, hop, u, later))
+            pl.when(~is_down)(lambda: self.hop(core, 0, hop, u, later))
+            pl.when(is_down)(lambda: self.hop(core, 1, hop, u, later))
 
         def run(core):
-            for hop in range(5, -1, -1):
-                at = t - 2 * hop
-                early = at < self.EARLY
-                u = jnp.where(early, at, at - self.LATER)
-                there = (at >= 0) & (u < self.total) & (early | (u >= self.EARLY))
-                pl.when(there)(functools.partial(both, core, hop, u))
+            for hop in range(4, -1, -1):
+                u = t - 2 * hop
+                pl.when((u >= 0) & (u < self.total))(functools.partial(both, core, hop, u))
 
         for core in (0, 1):
             pl.when(self.p.core == core)(functools.partial(run, core))
@@ -210,21 +197,20 @@
 
 
 def forward_kernel(x, dy, w_gate, w_up, w_down, gu, d, pq, act_out, at_out, h_out, dw_out,
-                   a, dyv, act, near, wt, wdt, pqs, h, ats, xs, dws, here, here_d, out_sem, in_sem, here_sem, own_sem,
-                   x_sem, dy_sem, act_sem, h_sem, w_sem, wd_sem, pq_sem, at_sem, xs_sem, dw_sem):
+                   a, dyv, act, wt, wdt, pqs, h, turned, xs, dws, here_gu, here_d, out_sem, in_sem, here_sem, own_sem,
+                   x_sem, dy_sem, act_sem, h_sem, at_sem, w_sem, wd_sem, pq_sem, xs_sem, dw_sem):
     tokens, width = a.shape
     n, m = act.shape[0], h.shape[0]
     p = Place()
-    gather = Gather(p, n, m, (None, here, here_d), (near, gu, d), (out_sem, in_sem, here_sem, own_sem))
+    gather = Gather(p, n, m, (here_gu, here_d), (gu, d), (out_sem, in_sem, here_sem, own_sem))
     copy = pltpu.make_async_copy
     copy(x, a, x_sem).start()
     for layer in range(2):
 
         def bring(j, c, layer=layer):
             u = j + layer * (n + m)
-            own = here.at[j] if layer else near.at[(j, *p.yz, p.core)]
-            copy(w_gate.at[layer, :, block(j)], own.at[pl.ds(0, 32)], here_sem.at[u]).start()
-            copy(w_up.at[layer, :, block(j)], own.at[pl.ds(32, 32)], here_sem.at[u]).start()
+            copy(w_gate.at[layer, :, block(j)], here_gu.at[layer * n + j, pl.ds(0, 32)], here_sem.at[u]).start()
+            copy(w_up.at[layer, :, block(j)], here_gu.at[layer * n + j, pl.ds(32, 32)], here_sem.at[u]).start()
             return c
 
         lax.fori_loop(0, n, bring, 0)
@@ -232,39 +218,33 @@
             u = n + i + layer * (n + m)
             copy(w_down.at[layer, :, pl.ds(i * TILE, TILE)], here_d.at[layer * m + i], here_sem.at[u]).start()
     copy(dy, dyv, dy_sem).start()
-    meet(p.neighbours(()))
-
-    def transposed(layer, i):
-        return copy(ats.at[lax.rem(i, 2)], at_out.at[layer, :, block(i)], at_sem.at[lax.rem(i, 2)])
+    meet(p.neighbours((FAR, HERE)))
 
     @scoped("norm")
-    def norm(layer, i, wide):
+    def norm(rows, wide):
         value = normed(wide)
-        a[block(i)] = value
-        pl.when(i >= 2)(lambda: transposed(layer, i - 2).wait())
-        ats[lax.rem(i, 2)] = value.T
-        transposed(layer, i).start()
-
-    def norm_done(layer):
-        for i in (tokens // TILE - 2, tokens // TILE - 1):
-            transposed(layer, i).wait()
+        a[rows] = value
+        turned[:, rows] = value.T
+
+    def turned_out(layer):
+        return copy(turned, at_out.at[layer], at_sem)
 
     def start(t, c):
         gather.step(t)
         pl.when(t == 1)(lambda: copy(x, a, x_sem).wait())
 
-        @pl.when((t >= 1) & (t <= tokens // TILE))
+        @pl.when(t >= 1)
         def _():
-            norm(0, t - 1, a[block(t - 1)].astype(F32))
+            norm(block(t - 1), a[block(t - 1)].astype(F32))
 
         return c
 
-    assert gather.done(0) >= tokens // TILE and gather.LATER == 4
-    lax.fori_loop(0, gather.done(0) + 1, start, 0)
-    norm_done(0)
-
-    def w_tile(j, k):
-        return copy(gu.at[j], wt.at[k], w_sem.at[k])
+    assert gather.done(0) == tokens // TILE
+    lax.fori_loop(0, gather.done(1), start, 0)
+    turned_out(0).start()
+
+    def w_tile(unit, k):
+        return copy(gu.at[unit], wt.at[k], w_sem.at[k])
 
     def wd_tile(i, k):
         return copy(d.at[i], wdt.at[k], wd_sem.at[k])
@@ -281,46 +261,58 @@
     def act_tile(j):
         return copy(act.at[j], act_out.at[j], act_sem)
 
-    base = gather.done(n + 1) + 2 * m
+    base = gather.done(n + m) + 1
 
     def hidden(layer):
         def body(j, c):
             k = lax.rem(j, 2)
             if layer:
-                gather.step(base + j)
+
+                def more(i, c):
+                    pl.when((i == 0) | (lax.rem(j, 3) == 2))(lambda: gather.step(base + j + lax.div(j, 3) + i))
+                    return c
+
+                lax.fori_loop(0, 2, more, 0)
             else:
-                first = jnp.where(j < 3, gather.done(0) + 1 + 3 * (j - 1), gather.done(2) + j - 2)
-
-                def more(i, c):
-                    pl.when((j > 0) & ((i == 0) | (j < 3)))(lambda: gather.step(first + i))
-                    return c
-
-                lax.fori_loop(0, 3, more, 0)
-            if layer:
-                pl.when(j < n - 1)(lambda: w_tile(j + 1, 1 - k).start())
-                w_tile(j, k).wait()
-            else:
+                gather.step(gather.done(1) + j)
+
+            @pl.when(j < n - 1)
+            def _():
+                w_tile(layer * n + j + 1, 1 - k).start()
+
+            if layer == 0:
 
                 @pl.when(j == n - 1)
                 def _():
-                    gather.step(gather.done(n))
                     wd_tile(0, 0).start()
                     x_tile(0, 0).start()
 
+            w_tile(layer * n + j, k).wait()
             pl.when(j >= 2 - 2 * layer)(lambda: pq_tile(layer, j, k).wait())
             if layer:
                 pl.when(j >= 2)(lambda: dw_tile(j - 2, k).wait())
-            with jax.named_scope("hidden"):
-                w = wt.at[k] if layer else near.at[j]
-                gate_w, up_w = (w[:, :, :, 32 * i : 32 * i + 32, :].reshape(width, TILE) for i in range(2))
+            gate_w, up_w = (wt[k, :, :, :, 32 * i : 32 * i + 32, :].reshape(width, TILE) for i in range(2))
+
+            @scoped("hidden")
+            def make(fresh):
                 for i in range(tokens // 512):
                     rows = pl.ds(512 * i, 512)
+                    if fresh:
+                        norm(rows, jnp.concatenate([h[q, rows] for q in range(m)], -1).astype(F32))
                     gate, up = dot(a[rows], gate_w), dot(a[rows], up_w)
                     s = 0.5 * jnp.tanh(0.5 * gate) + 0.5
                     silu = gate * s
                     pqs[k, 0, rows] = silu
                     pqs[k, 1, rows] = up * (s + silu * (1 - s))
                     act[j, rows] = (silu * up).astype(BF16)
+
+            if layer:
+                pl.when(j == 0)(lambda: make(True))
+                pl.when(j > 0)(lambda: make(False))
+                pl.when(j == 0)(lambda: turned_out(1).start())
+            else:
+                make(False)
+            pq_tile(layer, j, k).start()
             if layer:
 
                 @pl.when(j < n)
@@ -331,7 +323,6 @@
                 dw_tile(j, k).start()
             else:
                 act_tile(j).start()
-            pq_tile(layer, j, k).start()
             return c
 
         lax.fori_loop(0, n, body, 0)
@@ -339,7 +330,9 @@
             for j in (n - 2, n - 1):
                 pq_tile(layer, j, j % 2).wait()
                 dw_tile(j, j % 2).wait()
-
+            turned_out(1).wait()
+
+    w_tile(0, 0).start()
     hidden(0)
 
     def h_tile(i):
@@ -347,8 +340,7 @@
 
     def down(i, c):
         k = lax.rem(i, 2)
-        for more in range(2):
-            gather.step(gather.done(n + 1) + 2 * i + more)
+        gather.step(gather.done(n + 1) + i)
 
         @pl.when(i < m - 1)
         def _():
@@ -357,7 +349,7 @@
 
         @pl.when(i == m - 1)
         def _():
-            w_tile(0, 0).start()
+            w_tile(n, 0).start()
 
         with jax.named_scope("tiles"):
             wd_tile(i, k).wait()
@@ -372,17 +364,12 @@
 
     lax.fori_loop(0, m, down, 0)
 
-    def norm_later(i, c):
-        norm(1, i, jnp.concatenate([h[q, block(i)] for q in range(m)], -1).astype(F32))
-        return c
-
-    lax.fori_loop(0, tokens // TILE, norm_later, 0)
-    norm_done(1)
+    turned_out(0).wait()
     with jax.named_scope("between"):
         copy(act, act_out, act_sem).wait()
         copy(dy, dyv, dy_sem).wait()
     hidden(1)
-    gather.steps(base + n, max(0, gather.done(gather.total - 1) + 1 - base - n))
+    gather.steps(base + n + n // 3, max(0, gather.done(gather.total - 1) + 1 - (base + n + n // 3)))
     copy(h, h, h_sem).wait()
 
 
@@ -393,7 +380,7 @@
     n, m = hidden // TILE, width // TILE
     layers, pieces = 2, (4, 4, 2, 64, TILE)
     shapes = [
-        ((n, *pieces), BF16),
+        ((layers * n, *pieces), BF16),
         ((layers * m, hidden, TILE), BF16),
         ((layers * n, 2, tokens, TILE), F32),
         ((n, tokens, TILE), BF16),
@@ -412,22 +399,21 @@
         pltpu.VMEM((tokens, width), BF16),
         pltpu.VMEM((tokens, width), BF16),
         pltpu.VMEM((n, tokens, TILE), BF16),
-        pltpu.VMEM((n, *pieces), BF16),
         twice(*pieces),
         twice(hidden, TILE),
         twice(2, tokens, TILE, dtype=F32),
         pltpu.VMEM((m, tokens, TILE), BF16),
-        twice(width, TILE),
+        pltpu.VMEM((width, tokens), BF16),
         twice(tokens, TILE),
         twice(TILE, width),
-        pltpu.VMEM((n, *pieces[3:]), BF16),
+        pltpu.VMEM((layers * n, *pieces[3:]), BF16),
         pltpu.VMEM((layers * m, rows, TILE), BF16),
         sems(Gather.SLOTS, 3),
-        sems(Gather.SLOTS, 9),
+        sems(Gather.SLOTS, 8),
         sems(layers * (n + m)),
         sems(Gather.SLOTS),
     ]
-    scratch += [sems() for _ in range(4)] + [sems(2) for _ in range(6)]
+    scratch += [sems() for _ in range(5)] + [sems(2) for _ in range(5)]
     return pl.pallas_call(
         forward_kernel,
         out_shape=[jax.ShapeDtypeStruct(*shape) for shape in shapes],
@@ -457,16 +443,14 @@
             + many(slots, dtype=F32)
             + many(near, 3)
             + many(slots, 3)
-            + many(near, count=2)
-            + many(slots, count=2)
-            + [pltpu.SemaphoreType.DMA((slots, 10))] * 2
+            + many(slots, 4)
+            + [pltpu.SemaphoreType.DMA((slots, 11))] * 2
         )
 
     def __init__(self, p, refs, emit, lag, delay):
         self.p, self.emit, self.lag, self.delay = p, emit, lag, delay
         self.term, self.swapped, self.ca, self.cp, self.cm, self.x1, self.x2p, self.x2m, self.r1a, self.r1b, self.r2p, self.r2m = refs[:12]
-        self.db, self.y, self.ry, self.z, self.w, self.rz, self.rw = refs[12:19]
-        self.out_sem, self.in_sem = refs[19:]
+        self.db, self.y, self.ry, self.rx, self.out_sem, self.in_sem = refs[12:]
         self.half = self.term.shape[-1] // 2
 
     def slot(self, ref, u):
@@ -485,9 +469,8 @@
             y, ry = self.slot(self.y, u), self.slot(self.ry, u)
             return [one(5 + i, y.at[i], ry.at[i], p.at(HERE, ahead)) for i, ahead in enumerate(OTHERS)]
         if hop > 3:
-            second = hop == 5
-            src, dst = (self.w, self.rw) if second else (self.z, self.rz)
-            return [one(4 + hop, self.slot(src, u), self.slot(dst, u), p.pair(second))]
+            mine = self.slot(self.rx, u).at[p.x]
+            return [one(8 + i, mine, mine, p.along_x(d)) for i, d in enumerate(OTHERS)]
         sources, landings = ((self.x1, self.x1), (self.r1a, self.r1b)) if hop == 1 else ((self.x2p, self.x2m), (self.r2p, self.r2m))
         made = []
         for side, (src, dst, ahead) in enumerate(zip(sources, landings, (NEXT, LAST), strict=True)):
@@ -524,11 +507,9 @@
                 value = of(self.ca, e) + of(self.r2p, e) + of(self.r2m, e)
                 put(self.y, value, e - 1) if e else put(self.db, value)
         if hop == 4:
-            put(self.z, (of(self.db) + of(self.ry, 0)) + (of(self.ry, 1) + of(self.ry, 2)))
+            put(self.rx, (of(self.db) + of(self.ry, 0)) + (of(self.ry, 1) + of(self.ry, 2)), p.x)
         if hop == 5:
-            put(self.w, of(self.z) + of(self.rz))
-        if hop == 6:
-            self.emit(u, (of(self.w) + of(self.rw)).astype(BF16))
+            self.emit(u, ((of(self.rx, 0) + of(self.rx, 1)) + (of(self.rx, 2) + of(self.rx, 3))).astype(BF16))
 
     def hop(self, hop, u):
         with jax.named_scope(f"hop{hop}"):
@@ -608,7 +589,7 @@
                 sum_gu.step(first + j, first, first + n)
                 d_turn(j)
                 if layer:
-                    copy(gu.at[j], big.at[j], big_sem.at[0]).start()
+                    copy(gu.at[n + j], big.at[j], big_sem.at[0]).start()
 
                 @pl.when(j < n - 1)
                 def _():
@@ -691,7 +672,7 @@
         for one in rows_in(0, 0):
             one.start()
         with jax.named_scope("weights"):
-            copy(gu, big, big_sem.at[0]).wait()
+            copy(gu.at[pl.ds(n, n)], big, big_sem.at[0]).wait()
         lax.fori_loop(0, tokens // TILE, body, 0)
 
     def down(turned, made):
@@ -730,7 +711,7 @@
 
     @scoped("meet")
     def begin():
-        meet(p.neighbours(((HERE, FAR),)) + [p.pair(False), p.pair(True)])
+        meet(p.neighbours((HERE, FAR)) + [p.along_x(d) for d in OTHERS])
         copy(dy, dh, dh_sem).wait()
         copy(at.at[1], av, at_sem).wait()
 
@@ -749,7 +730,6 @@
 
     def rest(i, c):
         sum_gu.step(2 * n + i, n, 2 * n)
-        pl.when(i == 1)(lambda: d_step(dw0, (n + 1) // 2 + 2, m, lambda s: None))
         return c
 
     lax.fori_loop(0, 2 * HOPS + 1, rest, 0)
@@ -757,10 +737,10 @@
 
 def backward(dy, gu, d, pq, act, at, h, dw1):
     tokens, width = dy.shape
-    n, hidden = gu.shape[0], dw1.shape[0]
+    n, hidden = gu.shape[0] // 2, dw1.shape[0]
     rows, m = hidden // 32, width // TILE
-    gu = gu.reshape(n, tokens, TILE)
-    assert 32 * 64 == tokens and n + 2 == 3 * m + 3 and 2 * HOPS + 1 <= tokens // TILE + 2 * m
+    gu = gu.reshape(2 * n, tokens, TILE)
+    assert 32 * 64 == tokens and n == 3 * m + 1 and HOPS + m == (n + 5) // 2 and 2 * HOPS + 1 <= tokens // TILE + 2 * m
     any_space, vmem = pl.BlockSpec(memory_space=pl.ANY), pl.BlockSpec(memory_space=pltpu.VMEM)
     shapes = [((2, 32, hidden), BF16)] * 2 + [((2, rows, width), BF16), ((n, 2, tokens, TILE), BF16), ((hidden, width), BF16)]
     out = pl.pallas_call(

time: 393 us -> 374 us (0.952)
  Pallas kernels: 384 us -> 365 us
    pallas_call x1, Pallas kernels: 172 us -> 155 us  [forward(): pl.pallas_call(forward_kernel, out_shape=[jax.ShapeDtypeStruct(*shape) fo...]
where the time goes in v5:
time: 374 us
  Pallas kernels  365 us (98%)
  other arithmetic  8.12 us (2%)
    pallas_call x1, Pallas kernels, backward(): pl.pallas_call(backward_kernel, out_shape=[jax.ShapeDtypeStruct(*shape) f...  210 us
    pallas_call x1, Pallas kernels, forward(): pl.pallas_call(forward_kernel, out_shape=[jax.ShapeDtypeStruct(*shape) fo...  155 us
    convert_element_type x2, other arithmetic, adamw(): return ((w - 0.02 * step).astype(jnp.bfloat16), m, v)  8.12 us

profile of v5, /device:TPU:0, one launch (start us, length us, event | category | flops | bytes accessed | tf_op | source)
XLA Modules:
  0.0 374.1 jit_solution(2103714869522167829)
XLA Ops:
  0.6 155.0 %forward.1 = (bf16[26,4,4,2,64,256]{5,4,3,2,1,0:T(8,128)(2,1)}, bf16[8,3328,256]{2,1,0:T(8,128)(2,1)}, f32[26,2,2048,256]{3,2,1,0:T(8,128)}, bf16[13,2048,256]{2...) custom-call(bf16[2048,1024]{1,0:T(8,128)(2,1)} %bitcast.6, ...), custom_call_target="tpu_custom_call" | custom-call | tf_op jit(solution)/shard_map/forward/pallas_call | solution.py:417
  155.6 210.3 %backward.1 = (bf16[2,32,3328]{2,1,0:T(8,128)(2,1)}, bf16[2,32,3328]{2,1,0:T(8,128)(2,1)}, bf16[2,104,1024]{2,1,0:T(8,128)(2,1)}, bf16[13,2,2048,256]{3,2,1,0:T(8,128)(2,1)}, bf16[3328,1024]{1,0:T(8,128)(2,1)}) custom-call(bf16[2048,1024]{1,0:T(8,128)(2,1)} %bitcast.5, bf16[26,2048,256]{2,1,0:T(8,128)(2,1)} %bitcast.3, ...), custom_call_target="tpu_custom_call" | custom-call | tf_op jit(solution)/shard_map/backward/pallas_call | solution.py:746
  366.0 3.3 fusion.10
  369.2 4.9 %fusion.2 = (bf16[2,32,3328]{2,1,0:T(8,128)(2,1)}, f32[2,32,3328]{2,1,0:T(8,128)}, f32[2,32,3328]{2,1,0:T(8,128)}, bf16[2,32,3328]{2,1,0:T(8,128)(2,1)}, f32[2,32,3328]{2,1,0:T(8,128)}, /*index=5*/f32[2,32,3328]{2,1,0:T(8,128)}) fusion(bf16[2,32,3328]{2,1,0:T(8,128)(2,1)} %w_gate.1, bf16[2,32,3328]{2,1,0:T(8,128)(2,1)} %get-tuple-element.26, ...), kind=kLoop, calls=%fused_computation.14 | loop fusion | flops 6815744 | bytes 9371648 | tf_op jit(solution)/shard_map/convert_element_type | solution.py:24

commit v6 on v5

--- a/solution.py
+++ b/solution.py
@@ -22,6 +22,28 @@
     v = 0.95 * v + 0.05 * g * g
     step = m * lax.rsqrt(v + 1e-8) + 0.1 * w
     return (w - 0.02 * step).astype(jnp.bfloat16), m, v
+
+
+def update_kernel(*refs):
+    given, out = refs[:12], refs[12:]
+    for i in range(3):
+        new = adamw(*(ref[...].astype(F32) for ref in given[i::3]))
+        for ref, value in zip(out[i::3], new, strict=True):
+            ref[...] = value
+
+
+def update(weights, m, v, gradients):
+    def spec(w):
+        return pl.BlockSpec((1, w.shape[1], w.shape[2] // 2), lambda layer, half: (layer, 0, half))
+
+    return pl.pallas_call(
+        update_kernel,
+        grid=(2, 2),
+        out_shape=[jax.ShapeDtypeStruct(w.shape, w.dtype) for w in (*weights, *m, *v)],
+        in_specs=[spec(w) for w in weights] * 4,
+        out_specs=[spec(w) for w in weights] * 3,
+        name="update",
+    )(*weights, *m, *v, *gradients)
 
 
 def dot(a, b, dims=PLAIN):
@@ -268,8 +290,10 @@
             k = lax.rem(j, 2)
             if layer:
 
+                extra = jnp.maximum(lax.div(j - 7, 2), 0)
+
                 def more(i, c):
-                    pl.when((i == 0) | (lax.rem(j, 3) == 2))(lambda: gather.step(base + j + lax.div(j, 3) + i))
+                    pl.when((i == 0) | ((j > 7) & (lax.rem(j, 2) == 0)))(lambda: gather.step(base + j + extra + i))
                     return c
 
                 lax.fori_loop(0, 2, more, 0)
@@ -369,7 +393,7 @@
         copy(act, act_out, act_sem).wait()
         copy(dy, dyv, dy_sem).wait()
     hidden(1)
-    gather.steps(base + n + n // 3, max(0, gather.done(gather.total - 1) + 1 - (base + n + n // 3)))
+    gather.steps(base + n + 3, max(0, gather.done(gather.total - 1) + 1 - (base + n + 3)))
     copy(h, h, h_sem).wait()
 
 
@@ -551,6 +575,10 @@
     copy(at.at[1], av, at_sem).start()
 
     def d_start(term, s, first):
+        if len(term.shape) > 2:
+            copy(term.at[:, :, :, block(s)], sum_d.term.at[lax.rem(first + s, 2)], load_sem).start()
+            return
+
         def one(i, c):
             rows = pl.ds(pl.multiple_of(d_rows * i, 8), d_rows)
             copy(term.at[rows, block(s)], sum_d.term.at[lax.rem(first + s, 2), lax.div(i, 2), lax.rem(i, 2)], load_sem).start()
@@ -700,14 +728,16 @@
             out(e).start()
             return c
 
+        def columns():
+            lax.fori_loop(0, m, body, 0)
+            copy(at.at[0], av, at_sem).wait()
+
         copy(act, big, big_sem.at[0]).start()
-        lax.fori_loop(0, m, body, 0)
 
         def last_turn(j):
             pl.when(lax.rem(j, 2) == 0)(lambda: d_step(dw0, 2 + lax.div(j, 2), m, lambda s: out(s).wait()))
 
-        copy(at.at[0], av, at_sem).wait()
-        gradients(0, n, lambda: None, last_turn)
+        gradients(0, n, columns, last_turn)
 
     @scoped("meet")
     def begin():
@@ -755,16 +785,14 @@
         + Sum.scratch(2, 2, rows, TILE),
         compiler_params=pltpu.CompilerParams(collective_id=1, has_side_effects=True, vmem_limit_bytes=VMEM_LIMIT),
         name="backward",
-    )(dy, gu, d, pq, act, at, h, dw1)
+    )(dy, gu, d, pq, act, at, h, dw1.reshape(16, 2, rows, width))
     return out[:3]
 
 
 def solution(mesh):
     def step(x, dy, *arrays):
         weights, m, v = (arrays[i : i + 3] for i in (0, 3, 6))
-        gradients = backward(dy[0], *forward(x[0], dy[0], weights))
-        new = [adamw(w.astype(F32), m, v, g.astype(F32)) for w, m, v, g in zip(weights, m, v, gradients, strict=True)]
-        return tuple(one[which] for which in range(3) for one in new)
+        return tuple(update(weights, m, v, backward(dy[0], *forward(x[0], dy[0], weights))))
 
     states, cut = P(("rep", "r", "s"), None, None), P(None, "s", None)
     return jax.shard_map(

time: 374 us -> 367 us (0.981)
  other arithmetic: 8.12 us -> 0 us
    convert_element_type x2 -> x0, other arithmetic: 8.12 us -> none  [adamw(): return ((w - 0.02 * step).astype(jnp.bfloat16), m, v)]
    pallas_call x0 -> x1, Pallas kernels: none -> 6.43 us  [update(): pl.pallas_call(update_kernel, grid=(2, 2), out_shape=[jax.ShapeDtypeStruc...]
where the time goes in v6:
time: 367 us
  Pallas kernels  366 us (100%)
    pallas_call x1, Pallas kernels, backward(): pl.pallas_call(backward_kernel, out_shape=[jax.ShapeDtypeStruct(*shape) f...  208 us
    pallas_call x1, Pallas kernels, forward(): pl.pallas_call(forward_kernel, out_shape=[jax.ShapeDtypeStruct(*shape) fo...  151 us

profile of v6, /device:TPU:0, one launch (start us, length us, event | category | flops | bytes accessed | tf_op | source)
XLA Modules:
  0.0 366.9 jit_solution(14871164766867502110)
XLA Ops:
  0.6 151.3 %forward.1 = (bf16[26,4,4,2,64,256]{5,4,3,2,1,0:T(8,128)(2,1)}, bf16[8,3328,256]{2,1,0:T(8,128)(2,1)}, f32[26,2,2048,256]{3,2,1,0:T(8,128)}, bf16[13,2048,256]{2...) custom-call(bf16[2048,1024]{1,0:T(8,128)(2,1)} %bitcast.8, ...), custom_call_target="tpu_custom_call" | custom-call | tf_op jit(solution)/shard_map/forward/pallas_call | solution.py:441
  151.9 208.4 %backward.1 = (bf16[2,32,3328]{2,1,0:T(8,128)(2,1)}, bf16[2,32,3328]{2,1,0:T(8,128)(2,1)}, bf16[2,104,1024]{2,1,0:T(8,128)(2,1)}, bf16[13,2,2048,256]{3,2,1,0:T(8,128)(2,1)}, bf16[3328,1024]{1,0:T(8,128)(2,1)}) custom-call(bf16[2048,1024]{1,0:T(8,128)(2,1)} %bitcast.6, bf16[26,2048,256]{2,1,0:T(8,128)(2,1)} %bitcast.4, ...), custom_call_target="tpu_custom_call" | custom-call | tf_op jit(solution)/shard_map/backward/pallas_call | solution.py:776
  360.3 6.4 %update.1 = (bf16[2,32,3328]{2,1,0:T(8,128)(2,1)}, bf16[2,32,3328]{2,1,0:T(8,128)(2,1)}, bf16[2,104,1024]{2,1,0:T(8,128)(2,1)}, f32[2,32,3328]{2,1,0:T(8,128)}, ...) custom-call(bf16[2,32,3328]{2,1,0:T(8,128)(2,1)} %refs_0_.1, ...), custom_call_target="tpu_custom_call" | custom-call | tf_op jit(solution)/shard_map/update/pallas_call | solution.py:39

commit v7 on v6

--- a/solution.py
+++ b/solution.py
@@ -103,11 +103,11 @@
         return [self.partner()] + around
 
 
-def meet(places):
+def greet(places):
     barrier = pltpu.get_barrier_semaphore()
     for place in places:
         pl.semaphore_signal(barrier, inc=1, device_id=place, device_id_type=MESH)
-    pl.semaphore_wait(barrier, len(places))
+    return lambda: pl.semaphore_wait(barrier, len(places))
 
 
 def send(src, dst, send_sem, recv_sem, place):
@@ -225,6 +225,7 @@
     n, m = act.shape[0], h.shape[0]
     p = Place()
     gather = Gather(p, n, m, (here_gu, here_d), (gu, d), (out_sem, in_sem, here_sem, own_sem))
+    met = greet(p.neighbours((FAR, HERE)))
     copy = pltpu.make_async_copy
     copy(x, a, x_sem).start()
     for layer in range(2):
@@ -240,7 +241,7 @@
             u = n + i + layer * (n + m)
             copy(w_down.at[layer, :, pl.ds(i * TILE, TILE)], here_d.at[layer * m + i], here_sem.at[u]).start()
     copy(dy, dyv, dy_sem).start()
-    meet(p.neighbours((FAR, HERE)))
+    met()
 
     @scoped("norm")
     def norm(rows, wide):
@@ -560,6 +561,7 @@
     half = len(scratch) // 2
     copy = pltpu.make_async_copy
     p = Place()
+    met = greet(p.neighbours((HERE, FAR)) + [p.along_x(d) for d in OTHERS])
 
     def emit_gu(u, value):
         later = lax.div(u, n)
@@ -614,6 +616,8 @@
 
             def body(j, c):
                 k = lax.rem(j, 2)
+                if layer:
+                    pl.when(j == 1)(met)
                 sum_gu.step(first + j, first, first + n)
                 d_turn(j)
                 if layer:
@@ -670,7 +674,7 @@
         def body(i, c):
             k = lax.rem(i, 2)
             sum_gu.step(n + i, 0, n)
-            pl.when(k == 0)(lambda: d_step(dw1, (n + 1) // 2 + lax.div(i, 2), 0))
+            pl.when(k == 0)(lambda: d_step(dw1, n // 2 + lax.div(i, 2), 0))
 
             @pl.when(i < tokens // TILE - 1)
             def _():
@@ -741,14 +745,13 @@
 
     @scoped("meet")
     def begin():
-        meet(p.neighbours((HERE, FAR)) + [p.along_x(d) for d in OTHERS])
+        d_start(dw1, 0, 0)
         copy(dy, dh, dh_sem).wait()
         copy(at.at[1], av, at_sem).wait()
 
     def turn(j):
-        pl.when(lax.rem(j, 2) == 0)(lambda: d_step(dw1, lax.div(j, 2), 0))
-
-    d_start(dw1, 0, 0)
+        pl.when((lax.rem(j, 2) == 0) & (j > 0))(lambda: d_step(dw1, lax.div(j, 2) - 1, 0))
+
     gradients(1, 0, begin, turn)
     copy(at.at[0], av, at_sem).start()
     pl.run_scoped(

time: 367 us -> 368 us (level)
  no operation moved by 1% of the time
where the time goes in v7:
time: 368 us
  Pallas kernels  367 us (100%)
    pallas_call x1, Pallas kernels, backward(): pl.pallas_call(backward_kernel, out_shape=[jax.ShapeDtypeStruct(*shape) f...  210 us
    pallas_call x1, Pallas kernels, forward(): pl.pallas_call(forward_kernel, out_shape=[jax.ShapeDtypeStruct(*shape) fo...  151 us

profile of v7, /device:TPU:0, one launch (start us, length us, event | category | flops | bytes accessed | tf_op | source)
XLA Modules:
  0.0 368.1 jit_solution(12257850021061114975)
XLA Ops:
  0.6 151.1 %forward.1 = (bf16[26,4,4,2,64,256]{5,4,3,2,1,0:T(8,128)(2,1)}, bf16[8,3328,256]{2,1,0:T(8,128)(2,1)}, f32[26,2,2048,256]{3,2,1,0:T(8,128)}, bf16[13,2048,256]{2...) custom-call(bf16[2048,1024]{1,0:T(8,128)(2,1)} %bitcast.8, ...), custom_call_target="tpu_custom_call" | custom-call | tf_op jit(solution)/shard_map/forward/pallas_call | solution.py:442
  151.8 209.7 %backward.1 = (bf16[2,32,3328]{2,1,0:T(8,128)(2,1)}, bf16[2,32,3328]{2,1,0:T(8,128)(2,1)}, bf16[2,104,1024]{2,1,0:T(8,128)(2,1)}, bf16[13,2,2048,256]{3,2,1,0:T(8,128)(2,1)}, bf16[3328,1024]{1,0:T(8,128)(2,1)}) custom-call(bf16[2048,1024]{1,0:T(8,128)(2,1)} %bitcast.6, bf16[26,2048,256]{2,1,0:T(8,128)(2,1)} %bitcast.4, ...), custom_call_target="tpu_custom_call" | custom-call | tf_op jit(solution)/shard_map/backward/pallas_call | solution.py:779
  361.5 6.4 %update.1 = (bf16[2,32,3328]{2,1,0:T(8,128)(2,1)}, bf16[2,32,3328]{2,1,0:T(8,128)(2,1)}, bf16[2,104,1024]{2,1,0:T(8,128)(2,1)}, f32[2,32,3328]{2,1,0:T(8,128)}, ...) custom-call(bf16[2,32,3328]{2,1,0:T(8,128)(2,1)} %refs_0_.1, ...), custom_call_target="tpu_custom_call" | custom-call | tf_op jit(solution)/shard_map/update/pallas_call | solution.py:39

commit v8 on v6

--- a/solution.py
+++ b/solution.py
@@ -570,7 +570,7 @@
         later = lax.div(u, m)
         g_down[1 - later, :, block(u - m * later)] = value
 
-    sum_gu, sum_d = Sum(p, scratch[:half], emit_gu, 2, 1), Sum(p, scratch[half:], emit_d, 1, 0)
+    sum_gu, sum_d = Sum(p, scratch[:half], emit_gu, 2, 0), Sum(p, scratch[half:], emit_d, 1, 0)
     copy(dy, dh, dh_sem).start()
     copy(at.at[1], av, at_sem).start()
 
@@ -643,6 +643,7 @@
                             sum_gu.term[slot, 4 * i : 4 * i + 4, :, 32 * e : 32 * e + 32, :] = value.reshape(4, 2, 32, TILE)
                 if layer:
                     dgu_tile(j, k).start()
+                sum_gu.hop(0, first + j)
                 return c
 
             for one in tiles(0, 0):
@@ -762,7 +763,7 @@
         sum_gu.step(2 * n + i, n, 2 * n)
         return c
 
-    lax.fori_loop(0, 2 * HOPS + 1, rest, 0)
+    lax.fori_loop(0, 2 * HOPS, rest, 0)
 
 
 def backward(dy, gu, d, pq, act, at, h, dw1):

time: 367 us -> 366 us (level)
  no operation moved by 1% of the time
where the time goes in v8:
time: 366 us
  Pallas kernels  365 us (100%)
    pallas_call x1, Pallas kernels, backward(): pl.pallas_call(backward_kernel, out_shape=[jax.ShapeDtypeStruct(*shape) f...  207 us
    pallas_call x1, Pallas kernels, forward(): pl.pallas_call(forward_kernel, out_shape=[jax.ShapeDtypeStruct(*shape) fo...  151 us

profile of v8, /device:TPU:0, one launch (start us, length us, event | category | flops | bytes accessed | tf_op | source)
XLA Modules:
  0.0 365.7 jit_solution(16153637078661353544)
XLA Ops:
  0.6 151.3 %forward.1 = (bf16[26,4,4,2,64,256]{5,4,3,2,1,0:T(8,128)(2,1)}, bf16[8,3328,256]{2,1,0:T(8,128)(2,1)}, f32[26,2,2048,256]{3,2,1,0:T(8,128)}, bf16[13,2048,256]{2...) custom-call(bf16[2048,1024]{1,0:T(8,128)(2,1)} %bitcast.8, ...), custom_call_target="tpu_custom_call" | custom-call | tf_op jit(solution)/shard_map/forward/pallas_call | solution.py:441
  151.9 207.2 %backward.1 = (bf16[2,32,3328]{2,1,0:T(8,128)(2,1)}, bf16[2,32,3328]{2,1,0:T(8,128)(2,1)}, bf16[2,104,1024]{2,1,0:T(8,128)(2,1)}, bf16[13,2,2048,256]{3,2,1,0:T(8,128)(2,1)}, bf16[3328,1024]{1,0:T(8,128)(2,1)}) custom-call(bf16[2048,1024]{1,0:T(8,128)(2,1)} %bitcast.6, bf16[26,2048,256]{2,1,0:T(8,128)(2,1)} %bitcast.4, ...), custom_call_target="tpu_custom_call" | custom-call | tf_op jit(solution)/shard_map/backward/pallas_call | solution.py:777
  359.1 6.4 %update.1 = (bf16[2,32,3328]{2,1,0:T(8,128)(2,1)}, bf16[2,32,3328]{2,1,0:T(8,128)(2,1)}, bf16[2,104,1024]{2,1,0:T(8,128)(2,1)}, f32[2,32,3328]{2,1,0:T(8,128)}, ...) custom-call(bf16[2,32,3328]{2,1,0:T(8,128)(2,1)} %refs_0_.1, ...), custom_call_target="tpu_custom_call" | custom-call | tf_op jit(solution)/shard_map/update/pallas_call | solution.py:39
